TPU v7x, 256 devices: a whole 4x4x8 slice. The times are simulated.
256 devices in a mesh: north: 64 (over z_lo, y, x, core), east: 4 (over z_hi).
Axes of the slice: x: 4, y: 4, z: 8 (z_hi: 4, z_lo: 2; z = z_hi * 2 + z_lo), core: 2. Of those that a mesh axis runs over, the one named last changes fastest.
Arguments:
- right_side: float32 [4096, 256, 256], P('north', 'east'), may hold values from -6 to 6
- first_guess: float32 [4096, 256, 256], P('north', 'east'), may hold values from -6 to 6
- mass_term: float32 [4096, 256, 256], P('north', 'east'), may hold values from 0.1 to 0.9
Outputs:
- corrected: float32 [4096, 256, 256], P('north', 'east')
- remaining: float32 [4096, 256, 256], P('north', 'east')
All inputs are finite; a program needn't handle non-finite values.
Results may differ from a plain program's by a relative error of at most 0.000032.
Values sent between devices are 32-bit elements; how exact they have to be, the bound alone decides.
No kernel may reach another device: no remote copies, remote signals or barrier semaphores. Data moves between devices by JAX's collectives and lax.ppermute only.
A program may use at most 128 MiB of HBM per device.

v0:
```python
import jax
import jax.numpy as jnp
from jax import lax
from jax.experimental import pallas as pl
from jax.experimental.pallas import tpu as pltpu
from jax.sharding import PartitionSpec as P

NY, NX, NC = 64, 64, 256
HALVES = 2
LANES = 128
DEEP = 3
LEFT = 16
FY, FX = NY + 2 * DEEP, NX + 2 * LEFT
CY, CX = NY // 2, NX // 2
WIDE = 6
TOP = 8
GY, GX = CY + 20, CX + 2 * LEFT
BLOCK = 4

VMEM = pltpu.VMEM
F32 = jnp.float32
IN_VMEM = pl.BlockSpec(memory_space=VMEM)
IN_HBM = pl.BlockSpec(memory_space=pltpu.HBM)


def corner_cells(arrays):
    cells = []
    for k, (at, deep) in enumerate(arrays):
        for side in range(2):
            for dy in range(1, deep):
                cells.append((side, at + (deep - dy if side == 0 else dy - 1), deep - dy, k, dy))
    return cells


INPUTS = ((0, 3), (3, 2), (5, 2))
COARSE = ((0, WIDE), (WIDE, WIDE))
VALUES = ((0, 3),)


def half(c):
    return pl.ds(c * LANES, LANES)


def shape(*dims):
    return jax.ShapeDtypeStruct(dims, F32)


def exchange(low, high, axis):
    size = lax.axis_size(axis)
    up = [(i, (i + 1) % size) for i in range(size)]
    down = [(b, a) for a, b in up]
    return lax.ppermute(high, axis, up), lax.ppermute(low, axis, down)


def pack_kernel(cells, width, n_lo, n_hi, down, up):
    at = 0
    for side, row, n, _, _ in cells:
        src = (n_lo, n_hi)[side]
        down[pl.ds(at, n), :] = src[row, pl.ds(0, n), :]
        up[pl.ds(at, n), :] = src[row, pl.ds(width - n, n), :]
        at += n


def pack(cells, n_lo, n_hi):
    size = -(-sum(c[2] for c in cells) // 8) * 8
    return pl.pallas_call(
        lambda *refs: pack_kernel(cells, n_lo.shape[1], *refs),
        out_shape=(shape(size, NC),) * 2,
        in_specs=[IN_VMEM] * 2,
        out_specs=(IN_VMEM,) * 2,
        compiler_params=pltpu.CompilerParams(vmem_limit_bytes=8 * 2**20),
        name="pack",
    )(n_lo, n_hi)


def halos(arrays, east_low, east_high, north_low, north_high):
    e_lo, e_hi = exchange(east_low, east_high, "east")
    n_lo, n_hi = exchange(north_low, north_high, "north")
    down, up = pack(corner_cells(arrays), n_lo, n_hi)
    c_lo, c_hi = exchange(down, up, "east")
    return e_lo, e_hi, n_lo, n_hi, c_lo, c_hi


def edges_kernel(u_ref, f_ref, m_ref, el_ref, eh_ref, nl_ref, nh_ref, tiles, sems, row_sems):
    arrays = ((u_ref, 3, 0), (f_ref, 2, 3), (m_ref, 2, 5))
    copies = []
    rows = []
    for k, (ref, deep, at) in enumerate(arrays):
        for side in range(2):
            for c in range(HALVES):
                cp = pltpu.make_async_copy(
                    ref.at[:, pl.ds(side * (NX - 8), 8), half(c)],
                    tiles.at[k, side, c],
                    sems.at[k, side, c],
                )
                cp.start()
                copies.append((cp, k, side, c, deep, at))
            out = (nl_ref, nh_ref)[side]
            start = 0 if side == 0 else NY - deep
            cp = pltpu.make_async_copy(
                ref.at[pl.ds(start, deep)], out.at[pl.ds(at, deep)], row_sems.at[k, side]
            )
            cp.start()
            rows.append(cp)
    for cp, k, side, c, deep, at in copies:
        cp.wait()
        flat = tiles.at[k, side, c].reshape(NY * 8, LANES)
        out = (el_ref, eh_ref)[side]
        first = 0 if side == 0 else 8 - deep
        for d in range(deep):
            out[at + d, :, half(c)] = flat[pl.ds(first + d, NY, stride=8), :]
    for cp in rows:
        cp.wait()


def edges(u, f, m):
    return pl.pallas_call(
        edges_kernel,
        out_shape=(shape(7, NY, NC),) * 4,
        in_specs=[IN_HBM] * 3,
        out_specs=(IN_VMEM,) * 4,
        scratch_shapes=[
            VMEM((3, 2, HALVES, NY, 8, LANES), F32),
            pltpu.SemaphoreType.DMA((3, 2, HALVES)),
            pltpu.SemaphoreType.DMA((3, 2)),
        ],
        compiler_params=pltpu.CompilerParams(vmem_limit_bytes=16 * 2**20),
        name="edges",
    )(u, f, m)


def place_halo(dst, h, sizes, at, deep, array, cells, e_lo, e_hi, n_lo, n_hi, c_lo, c_hi):
    top, ny, nx, pitch = sizes
    cols = pl.ds(LEFT, nx)
    dst[pl.ds(top - deep, deep), cols, :] = n_lo[pl.ds(at, deep), :, h]
    dst[pl.ds(top + ny, deep), cols, :] = n_hi[pl.ds(at, deep), :, h]
    where = 0
    for side, _, n, k, dy in cells:
        if k == array:
            row = top - dy if side == 0 else top + ny + dy - 1
            dst[row, pl.ds(LEFT - n, n), :] = c_lo[pl.ds(where, n), h]
            dst[row, pl.ds(LEFT + nx, n), :] = c_hi[pl.ds(where, n), h]
        where += n
    flat = dst.reshape(dst.shape[0] * pitch, LANES)
    for d in range(deep):
        flat[pl.ds(top * pitch + LEFT - deep + d, ny, stride=pitch), :] = e_lo[at + d, :, h]
        flat[pl.ds(top * pitch + LEFT + nx + d, ny, stride=pitch), :] = e_hi[at + d, :, h]


FINE = (DEEP, NY, NX, FX)


def stencil(src, r, col, count, height):
    last = lax.broadcasted_iota(jnp.int32, (8, LANES), 0) == 7
    cache = {}

    def tile(k, t):
        if (k, t) not in cache:
            cache[k, t] = src[r + k, pl.ds(col + 8 * t, 8), :]
        return cache[k, t]

    turn = [pltpu.roll(tile(k, 0), 7, 0) for k in range(height)]
    for t in range(count):
        for k in range(height):
            following = pltpu.roll(tile(k, t + 1), 7, 0)
            right = jnp.where(last, following, turn[k])
            turn[k] = following
            left = src[r + k, pl.ds(col + 8 * t - 1, 8), :]
            yield k, t, tile(k, t), (tile(k - 1, t) + tile(k + 1, t)) + (left + right)


def sweep_rows(src, dst, load, weight, start, rows, col, count, mass=None):
    def block(i, carry):
        r = start + BLOCK * i
        for k, t, mid, s in stencil(src, r, col, count, BLOCK):
            at = pl.ds(col + 8 * t, 8)
            if mass is None:
                w = weight[r + k, at, :]
            else:
                w = 0.8 / (4.0 + mass[r + k, at, :])
                weight[r + k, at, :] = w
            dst[r + k, at, :] = 0.2 * mid + w * (s + load[r + k, at, :])
        return carry

    lax.fori_loop(0, rows // BLOCK, block, 0)


def two_sweeps(us, vs, fs, ms, ws):
    args = (1, NY + 4, LEFT - 8, NX // 8 + 2)
    sweep_rows(us, vs, fs, ws, *args, mass=ms)
    sweep_rows(vs, us, fs, ws, *args)


def fetch(refs, dsts, sems):
    copies = []
    for c in range(HALVES):
        copies.append([])
        for k, (ref, dst) in enumerate(zip(refs, dsts)):
            copy = pltpu.make_async_copy(
                ref.at[:, :, half(c)],
                dst.at[c, pl.ds(DEEP, NY), pl.ds(LEFT, NX), :],
                sems.at[c, k],
            )
            copy.start()
            copies[c].append(copy)
    return copies


def before_kernel(
    u_ref, f_ref, m_ref, e_lo, e_hi, n_lo, n_hi, c_lo, c_hi,
    u2_ref, cl_ref, cm_ref, cel, ceh, cnl, cnh, uel, ueh, unl, unh,
    us, fs, ms, ws, vs, pair, sems, out_sems,
):
    copies = fetch((u_ref, f_ref, m_ref), (us, fs, ms), sems)
    strips = (e_lo, e_hi, n_lo, n_hi, c_lo, c_hi)
    cells = corner_cells(INPUTS)
    outs = []
    for c in range(HALVES):
        h = half(c)
        u, f, m = us.at[c], fs.at[c], ms.at[c]
        for k, dst in enumerate((u, f, m)):
            place_halo(dst, h, FINE, *INPUTS[k], k, cells, *strips)
        for copy in copies[c]:
            copy.wait()
        two_sweeps(u, vs, f, m, ws)
        out = pltpu.make_async_copy(
            u.at[pl.ds(DEEP, NY), pl.ds(LEFT, NX), :], u2_ref.at[:, :, h], out_sems.at[c]
        )
        out.start()
        outs.append(out)

        def coarse_rows(i, carry):
            r = DEEP + 4 * i
            sums = {}
            for k, t, mid, s in stencil(u, r, LEFT, NX // 8, 4):
                at = pl.ds(LEFT + 8 * t, 8)
                mass = m[r + k, at, :]
                d = f[r + k, at, :] + s - (4.0 + mass) * mid
                if k % 2 == 0:
                    sums[t] = (d, mass)
                else:
                    pair[k // 2, 0, pl.ds(8 * t, 8), :] = sums[t][0] + d
                    pair[k // 2, 1, pl.ds(8 * t, 8), :] = sums[t][1] + mass
            for k in range(2):
                for which, ref in enumerate((cl_ref, cm_ref)):
                    ref[2 * i + k, :, h] = 0.5 * (
                        pair[k, which, pl.ds(0, CX, stride=2), :]
                        + pair[k, which, pl.ds(1, CX, stride=2), :]
                    )
            return carry

        lax.fori_loop(0, NY // 4, coarse_rows, 0)
        flat = u.reshape(FY * FX, LANES)
        for d in range(3):
            uel[d, :, h] = flat[pl.ds(DEEP * FX + LEFT + d, NY, stride=FX), :]
            ueh[d, :, h] = flat[pl.ds(DEEP * FX + LEFT + NX - 3 + d, NY, stride=FX), :]
            unl[d, :, h] = u[DEEP + d, pl.ds(LEFT, NX), :]
            unh[d, :, h] = u[NY + d, pl.ds(LEFT, NX), :]
    for d in range(WIDE):
        for k, ref in enumerate((cl_ref, cm_ref)):
            cel[k * WIDE + d] = ref[:, d, :]
            ceh[k * WIDE + d] = ref[:, CX - WIDE + d, :]
            cnl[k * WIDE + d] = ref[d]
            cnh[k * WIDE + d] = ref[CY - WIDE + d]
    for out in outs:
        out.wait()


def fine_scratch():
    both = VMEM((HALVES, FY, FX, LANES), F32)
    return [both] * 3 + [VMEM((FY, FX, LANES), F32)] * 2


def before(u, f, m, strips):
    return pl.pallas_call(
        before_kernel,
        out_shape=(shape(NY, NX, NC),)
        + (shape(CY, CX, NC),) * 2
        + (shape(2 * WIDE, CY, NC),) * 4
        + (shape(3, NY, NC),) * 4,
        in_specs=[IN_HBM] * 3 + [IN_VMEM] * 6,
        out_specs=(IN_HBM,) + (IN_VMEM,) * 10,
        scratch_shapes=fine_scratch()
        + [
            VMEM((2, 2, NX, LANES), F32),
            pltpu.SemaphoreType.DMA((HALVES, 3)),
            pltpu.SemaphoreType.DMA((HALVES,)),
        ],
        compiler_params=pltpu.CompilerParams(vmem_limit_bytes=40 * 2**20),
        name="before",
    )(u, f, m, *strips)


def coarse_kernel(
    cl_ref, cm_ref, e_lo, e_hi, n_lo, n_hi, c_lo, c_hi, uel, ueh, unl, unh,
    e_ref, ael, aeh, anl, anh,
    ls, ws, es, gs, tmp,
):
    cells = corner_cells(COARSE)
    rows, cols = pl.ds(TOP, CY), pl.ds(LEFT, CX)
    for c in range(HALVES):
        h = half(c)
        for k, (dst, ref) in enumerate(((ls, cl_ref), (ws, cm_ref))):
            dst[rows, cols, :] = ref[:, :, h]
            place_halo(
                dst, h, (TOP, CY, CX, GX), *COARSE[k], k, cells, e_lo, e_hi, n_lo, n_hi, c_lo, c_hi
            )
        wide = pl.ds(LEFT - 8, CX + 16)

        def first(i, carry):
            for k in range(BLOCK):
                r = TOP - WIDE + BLOCK * i + k
                w = 0.8 / (4.0 + ws[r, wide, :])
                ws[r, wide, :] = w
                es[r, wide, :] = w * ls[r, wide, :]
            return carry

        lax.fori_loop(0, (CY + 2 * WIDE) // BLOCK, first, 0)
        src, dst = es, gs
        for sweep in range(6):
            ring = 5 - sweep
            count = -(-(CY + 2 * ring) // BLOCK) * BLOCK
            sweep_rows(src, dst, ls, ws, TOP - ring, count, LEFT - 8, CX // 8 + 2)
            src, dst = dst, src
        e_ref[:, :, h] = src[rows, cols, :]
        flat = src.reshape(GY * GX, LANES)

        def spread(line):
            tmp[pl.ds(0, CX, stride=2), :] = line
            tmp[pl.ds(1, CX, stride=2), :] = line
            return tmp[...]

        for d in range(3):
            for out, old, x in ((ael, uel, d), (aeh, ueh, NX - 3 + d)):
                col = flat[pl.ds(TOP * GX + LEFT + x // 2, CY, stride=GX), :]
                out[d, :, h] = old[d, :, h] + spread(col)
            for out, old, y in ((anl, unl, d), (anh, unh, NY - 3 + d)):
                out[d, :, h] = old[d, :, h] + spread(src[TOP + y // 2, cols, :])


def coarse(load, mass, strips, u_strips):
    return pl.pallas_call(
        coarse_kernel,
        out_shape=(shape(CY, CX, NC),) + (shape(3, NY, NC),) * 4,
        in_specs=[IN_VMEM] * 12,
        out_specs=(IN_VMEM,) * 5,
        scratch_shapes=[VMEM((GY, GX, LANES), F32)] * 4 + [VMEM((NY, LANES), F32)],
        compiler_params=pltpu.CompilerParams(vmem_limit_bytes=24 * 2**20),
        name="coarse",
    )(load, mass, *strips, *u_strips)


def after_kernel(
    u_ref, f_ref, m_ref, e_ref, e_lo, e_hi, n_lo, n_hi, c_lo, c_hi,
    h_el, h_eh, h_nl, h_nh, h_cl, h_ch,
    out_ref, rest_ref,
    us, fs, ms, ws, vs, tmp, sems, out_sems,
):
    copies = fetch((u_ref, f_ref, m_ref), (us, fs, ms), sems)
    old = (h_el, h_eh, h_nl, h_nh, h_cl, h_ch)
    cells = corner_cells(INPUTS)
    outs = []
    for c in range(HALVES):
        h = half(c)
        u, f, m = us.at[c], fs.at[c], ms.at[c]
        mid = pl.ds(LEFT, NX)
        place_halo(
            u, h, FINE, *VALUES[0], 0, corner_cells(VALUES), e_lo, e_hi, n_lo, n_hi, c_lo, c_hi
        )
        for k, dst in ((1, f), (2, m)):
            place_halo(dst, h, FINE, *INPUTS[k], k, cells, *old)
        for copy in copies[c]:
            copy.wait()

        def add(i, carry):
            for k in range(4):
                line = e_ref[4 * i + k, :, h]
                tmp[k, pl.ds(0, CX, stride=2), :] = line
                tmp[k, pl.ds(1, CX, stride=2), :] = line
            for k in range(4):
                t = tmp[k]
                for j in range(2):
                    r = DEEP + 8 * i + 2 * k + j
                    u[r, mid, :] = u[r, mid, :] + t
            return carry

        lax.fori_loop(0, CY // 4, add, 0)
        two_sweeps(u, vs, f, m, ws)
        block = (pl.ds(DEEP, NY), mid)
        out = pltpu.make_async_copy(
            u.at[block[0], block[1], :], out_ref.at[:, :, h], out_sems.at[c, 0]
        )
        out.start()
        outs.append(out)

        def rest(i, carry):
            r = DEEP + BLOCK * i
            for k, t, value, s in stencil(u, r, LEFT, NX // 8, BLOCK):
                at = pl.ds(LEFT + 8 * t, 8)
                f[r + k, at, :] = f[r + k, at, :] + s - (4.0 + m[r + k, at, :]) * value
            return carry

        lax.fori_loop(0, NY // BLOCK, rest, 0)
        out = pltpu.make_async_copy(
            f.at[block[0], block[1], :], rest_ref.at[:, :, h], out_sems.at[c, 1]
        )
        out.start()
        outs.append(out)
    for out in outs:
        out.wait()


def after(u, f, m, e, strips, old):
    return pl.pallas_call(
        after_kernel,
        out_shape=(shape(NY, NX, NC),) * 2,
        in_specs=[IN_HBM] * 3 + [IN_VMEM] * 13,
        out_specs=(IN_HBM,) * 2,
        scratch_shapes=fine_scratch()
        + [
            VMEM((4, NX, LANES), F32),
            pltpu.SemaphoreType.DMA((HALVES, 3)),
            pltpu.SemaphoreType.DMA((HALVES, 2)),
        ],
        compiler_params=pltpu.CompilerParams(vmem_limit_bytes=40 * 2**20),
        name="after",
    )(u, f, m, e, *strips, *old)


def body(right_side, first_guess, mass_term):
    f, u, m = right_side, first_guess, mass_term
    old = halos(INPUTS, *edges(u, f, m))
    u2, load, mass, cel, ceh, cnl, cnh, *u_strips = before(u, f, m, old)
    wide = halos(COARSE, cel, ceh, cnl, cnh)
    e, *edge_values = coarse(load, mass, wide, u_strips)
    return after(u2, f, m, e, halos(VALUES, *edge_values), old)


def solution(mesh):
    spec = P("north", "east", None)
    return jax.shard_map(
        body, mesh=mesh, in_specs=(spec,) * 3, out_specs=(spec, spec), check_vma=False
    )
```

profile of v0, /device:TPU:0, one launch (start us, length us, event | category | flops | bytes accessed | tf_op | source)
XLA Modules:
  0.0 124.1 jit_solution(5881333344538672517)
XLA Ops:
  0.6 2.2 %copy-done = f32[64,64,256]{2,1,0:T(8,128)S(1)} copy-done((f32[64,64,256]{2,1,0:T(8,128)S(1)}, f32[64,64,256]{2,1,0:T(8,128)}, u32[]{:S(2)}) %copy-start) | copy-done | bytes 4194328
  2.8 2.2 %copy-done.2 = f32[64,64,256]{2,1,0:T(8,128)S(1)} copy-done((f32[64,64,256]{2,1,0:T(8,128)S(1)}, f32[64,64,256]{2,1,0:T(8,128)}, u32[]{:S(2)}) %copy-start.2) | copy-done | bytes 4194328
  5.0 2.2 %copy-done.3 = f32[64,64,256]{2,1,0:T(8,128)S(1)} copy-done((f32[64,64,256]{2,1,0:T(8,128)S(1)}, f32[64,64,256]{2,1,0:T(8,128)}, u32[]{:S(2)}) %copy-start.3) | copy-done | bytes 4194328
  7.2 2.0 %edges.1 = (f32[7,64,256]{2,1,0:T(8,128)S(1)}, f32[7,64,256]{2,1,0:T(8,128)S(1)}, f32[7,64,256]{2,1,0:T(8,128)S(1)}, f32[7,64,256]{2,1,0:T(8,128)S(1)}) custom-call(f32[64,64,256]{2,1,0:T(8,128)S(1)} %copy-done.3, f32[64,64,256]{2,1,0:T(8,128)S(1)} %copy-done, f32[64,64,256]{2,1,0:T(8,128)S(1)} %copy-done.2), custom_call_target="tpu_custom_call" | custom-call | tf_op jit(solution)/shard_map/edges/pallas_call | solution.py:117
  9.3 6.0 %collective-permute-start.3 = (f32[7,64,256]{2,1,0:T(8,128)S(1)}, f32[7,64,256]{2,1,0:T(8,128)S(1)}, u32[]{:S(2)}, u32[]{:S(2)}) collective-permute-start(f32[7,64,256]{2,1,0:T(8,128)S(1)} %get-tuple-element.31), channel_id=1, source_target_pairs={{4,0},{8,4},{12,8},{16,12},{20,16},{24,20},{28,24},{32,28},{36,32}... | collective-permute-start | bytes 1376264 | tf_op jit(solution)/shard_map/ppermute | solution.py:52
  15.2 1.7 %collective-permute-start = (f32[7,64,256]{2,1,0:T(8,128)S(1)}, f32[7,64,256]{2,1,0:T(8,128)S(1)}, u32[]{:S(2)}, u32[]{:S(2)}) collective-permute-start(f32[7,64,256]{2,1,0:T(8,128)S(1)} %get-tuple-element.28), channel_id=1, source_target_pairs={{0,1},{1,2},{2,3},{3,0},{4,5},{5,6},{6,7},{7,4},{8,9},{9,10},{10,1... | collective-permute-start | bytes 1376264 | tf_op jit(solution)/shard_map/ppermute | solution.py:52
  16.9 2.9 %collective-permute-start.1 = (f32[7,64,256]{2,1,0:T(8,128)S(1)}, f32[7,64,256]{2,1,0:T(8,128)S(1)}, u32[]{:S(2)}, u32[]{:S(2)}) collective-permute-start(f32[7,64,256]{2,1,0:T(8,128)S(1)} %get-tuple-element.29), channel_id=1, source_target_pairs={{1,0},{2,1},{3,2},{0,3},{5,4},{6,5},{7,6},{4,7},{9,8},{10,9},{11,1... | collective-permute-start | bytes 1376264 | tf_op jit(solution)/shard_map/ppermute | solution.py:52
  19.8 2.8 %collective-permute-done.2.refs_0_.n_lo.h_nl = f32[7,64,256]{2,1,0:T(8,128)S(1)} collective-permute-done((f32[7,64,256]{2,1,0:T(8,128)S(1)}, f32[7,64,256]{2,1,0:T(8,128)S(1)}, u32[]{:S(2)}, u32[]{:S(2)}) %collective-permute-start.2) | collective-permute-done | bytes 458784 | tf_op jit(solution)/shard_map/ppermute | solution.py:52
  22.6 10.0 %collective-permute-done.3.refs_1_.n_hi.h_nh = f32[7,64,256]{2,1,0:T(8,128)S(1)} collective-permute-done((f32[7,64,256]{2,1,0:T(8,128)S(1)}, f32[7,64,256]{2,1,0:T(8,128)S(1)}, u32[]{:S(2)}, u32[]{:S(2)}) %collective-permute-start.3) | collective-permute-done | bytes 458784 | tf_op jit(solution)/shard_map/ppermute | solution.py:52
  32.6 4.4 %collective-permute-start.4 = (f32[16,256]{1,0:T(8,128)S(1)}, f32[16,256]{1,0:T(8,128)S(1)}, u32[]{:S(2)}, u32[]{:S(2)}) collective-permute-start(f32[16,256]{1,0:T(8,128)S(1)} %get-tuple-element.32), channel_id=1, source_target_pairs={{0,1},{1,2},{2,3},{3,0},{4,5},{5,6},{6,7},{7,4},{8,9},{9,10},{10,1... | collective-permute-start | bytes 49160 | tf_op jit(solution)/shard_map/ppermute | solution.py:52
  37.0 1.1 collective-permute-start.5
  38.1 3.2 %collective-permute-done.e_lo.h_el = f32[7,64,256]{2,1,0:T(8,128)S(1)} collective-permute-done((f32[7,64,256]{2,1,0:T(8,128)S(1)}, f32[7,64,256]{2,1,0:T(8,128)S(1)}, u32[]{:S(2)}, u32[]{:S(2)}) %collective-permute-start) | collective-permute-done | bytes 458784 | tf_op jit(solution)/shard_map/ppermute | solution.py:52
  41.4 0.2 collective-permute-done.4.c_lo.h_cl
  41.6 1.7 %collective-permute-done.5.c_hi.h_ch = f32[16,256]{1,0:T(8,128)S(1)} collective-permute-done((f32[16,256]{1,0:T(8,128)S(1)}, f32[16,256]{1,0:T(8,128)S(1)}, u32[]{:S(2)}, u32[]{:S(2)}) %collective-permute-start.5) | collective-permute-done | bytes 16416 | tf_op jit(solution)/shard_map/ppermute | solution.py:52
  43.3 10.6 %before.1 = (f32[64,64,256]{2,1,0:T(8,128)S(1)}, f32[32,32,256]{2,1,0:T(8,128)S(1)}, f32[32,32,256]{2,1,0:T(8,128)S(1)}, f32[12,32,256]{2,1,0:T(8,128)S(1)}, f32...) custom-call(f32[64,64,256]{2,1,0:T(8,128)} %u_ref.3, ...), custom_call_target="tpu_custom_call" | custom-call | tf_op jit(solution)/shard_map/before/pallas_call | solution.py:275
  53.9 6.0 %collective-permute-start.9 = (f32[12,32,256]{2,1,0:T(8,128)S(1)}, f32[12,32,256]{2,1,0:T(8,128)S(1)}, u32[]{:S(2)}, u32[]{:S(2)}) collective-permute-start(f32[12,32,256]{2,1,0:T(8,128)S(1)} %get-tuple-element.40), channel_id=1, source_target_pairs={{4,0},{8,4},{12,8},{16,12},{20,16},{24,20},{28,24},{32,28},{36,32}... | collective-permute-start | bytes 1179656 | tf_op jit(solution)/shard_map/ppermute | solution.py:52
  59.9 3.1 %collective-permute-start.6 = (f32[12,32,256]{2,1,0:T(8,128)S(1)}, f32[12,32,256]{2,1,0:T(8,128)S(1)}, u32[]{:S(2)}, u32[]{:S(2)}) collective-permute-start(f32[12,32,256]{2,1,0:T(8,128)S(1)} %get-tuple-element.37), channel_id=1, source_target_pairs={{0,1},{1,2},{2,3},{3,0},{4,5},{5,6},{6,7},{7,4},{8,9},{9,10},{10,1... | collective-permute-start | bytes 1179656 | tf_op jit(solution)/shard_map/ppermute | solution.py:52
  63.0 1.0 collective-permute-start.7
  64.0 12.7 %collective-permute-done.8.refs_0_.n_lo = f32[12,32,256]{2,1,0:T(8,128)S(1)} collective-permute-done((f32[12,32,256]{2,1,0:T(8,128)S(1)}, f32[12,32,256]{2,1,0:T(8,128)S(1)}, u32[]{:S(2)}, u32[]{:S(2)}) %collective-permute-start.8) | collective-permute-done | bytes 393248 | tf_op jit(solution)/shard_map/ppermute | solution.py:52
  76.8 4.7 %collective-permute-start.10 = (f32[64,256]{1,0:T(8,128)S(1)}, f32[64,256]{1,0:T(8,128)S(1)}, u32[]{:S(2)}, u32[]{:S(2)}) collective-permute-start(f32[64,256]{1,0:T(8,128)S(1)} %get-tuple-element.41), channel_id=1, source_target_pairs={{0,1},{1,2},{2,3},{3,0},{4,5},{5,6},{6,7},{7,4},{8,9},{9,10},{10,1... | collective-permute-start | bytes 196616 | tf_op jit(solution)/shard_map/ppermute | solution.py:52
  81.4 0.2 collective-permute-start.11
  81.6 2.7 %collective-permute-done.10.c_lo = f32[64,256]{1,0:T(8,128)S(1)} collective-permute-done((f32[64,256]{1,0:T(8,128)S(1)}, f32[64,256]{1,0:T(8,128)S(1)}, u32[]{:S(2)}, u32[]{:S(2)}) %collective-permute-start.10) | collective-permute-done | bytes 65568 | tf_op jit(solution)/shard_map/ppermute | solution.py:52
  84.3 3.0 %collective-permute-done.11.c_hi = f32[64,256]{1,0:T(8,128)S(1)} collective-permute-done((f32[64,256]{1,0:T(8,128)S(1)}, f32[64,256]{1,0:T(8,128)S(1)}, u32[]{:S(2)}, u32[]{:S(2)}) %collective-permute-start.11) | collective-permute-done | bytes 65568 | tf_op jit(solution)/shard_map/ppermute | solution.py:52
  87.3 6.0 %coarse.1 = (f32[32,32,256]{2,1,0:T(8,128)S(1)}, f32[3,64,256]{2,1,0:T(8,128)S(1)}, f32[3,64,256]{2,1,0:T(8,128)S(1)}, f32[3,64,256]{2,1,0:T(8,128)S(1)}, f32[3,64,256]{2,1,0:T(8,128)S(1)}) custom-call(f32[32,32,256]{2,1,0:T(8,128)S(1)} %get-tuple-element.35.cl_ref, f32[32,32,256]{2,1,0:T(8,128)S(1)} %get-tuple-element.36.cm_ref, ...), custom_call_target="tpu_custom_call" | custom-call | tf_op jit(solution)/shard_map/coarse/pallas_call | solution.py:342
  93.4 6.0 %collective-permute-start.15 = (f32[3,64,256]{2,1,0:T(8,128)S(1)}, f32[3,64,256]{2,1,0:T(8,128)S(1)}, u32[]{:S(2)}, u32[]{:S(2)}) collective-permute-start(f32[3,64,256]{2,1,0:T(8,128)S(1)} %get-tuple-element.51), channel_id=1, source_target_pairs={{4,0},{8,4},{12,8},{16,12},{20,16},{24,20},{28,24},{32,28},{36,32}... | collective-permute-start | bytes 589832 | tf_op jit(solution)/shard_map/ppermute | solution.py:52
  99.3 1.0 collective-permute-start.12
  100.3 3.1 %collective-permute-start.13 = (f32[3,64,256]{2,1,0:T(8,128)S(1)}, f32[3,64,256]{2,1,0:T(8,128)S(1)}, u32[]{:S(2)}, u32[]{:S(2)}) collective-permute-start(f32[3,64,256]{2,1,0:T(8,128)S(1)} %get-tuple-element.49), channel_id=1, source_target_pairs={{1,0},{2,1},{3,2},{0,3},{5,4},{6,5},{7,6},{4,7},{9,8},{10,9},{11,1... | collective-permute-start | bytes 589832 | tf_op jit(solution)/shard_map/ppermute | solution.py:52
  103.5 4.4 %collective-permute-done.14.refs_0_.n_lo = f32[3,64,256]{2,1,0:T(8,128)S(1)} collective-permute-done((f32[3,64,256]{2,1,0:T(8,128)S(1)}, f32[3,64,256]{2,1,0:T(8,128)S(1)}, u32[]{:S(2)}, u32[]{:S(2)}) %collective-permute-start.14) | collective-permute-done | bytes 196640 | tf_op jit(solution)/shard_map/ppermute | solution.py:52
  107.9 1.4 %collective-permute-start.16 = (f32[8,256]{1,0:T(8,128)S(1)}, f32[8,256]{1,0:T(8,128)S(1)}, u32[]{:S(2)}, u32[]{:S(2)}) collective-permute-start(f32[8,256]{1,0:T(8,128)S(1)} %get-tuple-element.52), channel_id=1, source_target_pairs={{0,1},{1,2},{2,3},{3,0},{4,5},{5,6},{6,7},{7,4},{8,9},{9,10},{10,1... | collective-permute-start | bytes 24584 | tf_op jit(solution)/shard_map/ppermute | solution.py:52
  109.3 2.8 %collective-permute-start.17 = (f32[8,256]{1,0:T(8,128)S(1)}, f32[8,256]{1,0:T(8,128)S(1)}, u32[]{:S(2)}, u32[]{:S(2)}) collective-permute-start(f32[8,256]{1,0:T(8,128)S(1)} %get-tuple-element.53), channel_id=1, source_target_pairs={{1,0},{2,1},{3,2},{0,3},{5,4},{6,5},{7,6},{4,7},{9,8},{10,9},{11,1... | collective-permute-start | bytes 24584 | tf_op jit(solution)/shard_map/ppermute | solution.py:52
  112.1 1.6 %collective-permute-done.16.c_lo = f32[8,256]{1,0:T(8,128)S(1)} collective-permute-done((f32[8,256]{1,0:T(8,128)S(1)}, f32[8,256]{1,0:T(8,128)S(1)}, u32[]{:S(2)}, u32[]{:S(2)}) %collective-permute-start.16) | collective-permute-done | bytes 8224 | tf_op jit(solution)/shard_map/ppermute | solution.py:52
  113.8 10.1 %after.1 = (f32[64,64,256]{2,1,0:T(8,128)}, f32[64,64,256]{2,1,0:T(8,128)}) custom-call(f32[64,64,256]{2,1,0:T(8,128)S(1)} %get-tuple-element.34.u_ref, f32[64,64,256]{2,1,0:T(8,128)S(1)} %copy-done.1, f32[64,64,256]{2,1,0:T(8,128)} %m_ref.5, f32[32,32,256]{2,1,0:T(8,128)S(1)} %get-tuple-element.47.e_ref, f32[3,64,256]{2,1,0:T(8,128)S(1)} %collective-permute-done.12.e_lo, ...), custom_call_target="tpu_custom_call" | custom-call | tf_op jit(solution)/shard_map/after/pallas_call | solution.py:414
  (19 shorter events, 0.4 us)
Async XLA Ops:
  0.6 2.2 %copy-start = (f32[64,64,256]{2,1,0:T(8,128)S(1)}, f32[64,64,256]{2,1,0:T(8,128)}, u32[]{:S(2)}) copy-start(f32[64,64,256]{2,1,0:T(8,128)} %f_ref.5) | copy-start | bytes 12582916
  2.8 2.2 %copy-start.2 = (f32[64,64,256]{2,1,0:T(8,128)S(1)}, f32[64,64,256]{2,1,0:T(8,128)}, u32[]{:S(2)}) copy-start(f32[64,64,256]{2,1,0:T(8,128)} %m_ref.5) | copy-start | bytes 12582916
  5.0 2.2 %copy-start.3 = (f32[64,64,256]{2,1,0:T(8,128)S(1)}, f32[64,64,256]{2,1,0:T(8,128)}, u32[]{:S(2)}) copy-start(f32[64,64,256]{2,1,0:T(8,128)} %u_ref.3) | copy-start | bytes 12582916
  9.2 13.5 %collective-permute-start.2 = (f32[7,64,256]{2,1,0:T(8,128)S(1)}, f32[7,64,256]{2,1,0:T(8,128)S(1)}, u32[]{:S(2)}, u32[]{:S(2)}) collective-permute-start(f32[7,64,256]{2,1,0:T(8,128)S(1)} %get-tuple-element.30), channel_id=1, source_target_pairs={{0,4},{4,8},{8,12},{12,16},{16,20},{20,24},{24,28},{28,32},{32,36}... | collective-permute-start | bytes 1376264 | tf_op jit(solution)/shard_map/ppermute | solution.py:52
  9.3 23.3 %collective-permute-start.3 = (f32[7,64,256]{2,1,0:T(8,128)S(1)}, f32[7,64,256]{2,1,0:T(8,128)S(1)}, u32[]{:S(2)}, u32[]{:S(2)}) collective-permute-start(f32[7,64,256]{2,1,0:T(8,128)S(1)} %get-tuple-element.31), channel_id=1, source_target_pairs={{4,0},{8,4},{12,8},{16,12},{20,16},{24,20},{28,24},{32,28},{36,32}... | collective-permute-start | bytes 1376264 | tf_op jit(solution)/shard_map/ppermute | solution.py:52
  15.2 26.1 %collective-permute-start = (f32[7,64,256]{2,1,0:T(8,128)S(1)}, f32[7,64,256]{2,1,0:T(8,128)S(1)}, u32[]{:S(2)}, u32[]{:S(2)}) collective-permute-start(f32[7,64,256]{2,1,0:T(8,128)S(1)} %get-tuple-element.28), channel_id=1, source_target_pairs={{0,1},{1,2},{2,3},{3,0},{4,5},{5,6},{6,7},{7,4},{8,9},{9,10},{10,1... | collective-permute-start | bytes 1376264 | tf_op jit(solution)/shard_map/ppermute | solution.py:52
  16.9 24.5 %collective-permute-start.1 = (f32[7,64,256]{2,1,0:T(8,128)S(1)}, f32[7,64,256]{2,1,0:T(8,128)S(1)}, u32[]{:S(2)}, u32[]{:S(2)}) collective-permute-start(f32[7,64,256]{2,1,0:T(8,128)S(1)} %get-tuple-element.29), channel_id=1, source_target_pairs={{1,0},{2,1},{3,2},{0,3},{5,4},{6,5},{7,6},{4,7},{9,8},{10,9},{11,1... | collective-permute-start | bytes 1376264 | tf_op jit(solution)/shard_map/ppermute | solution.py:52
  32.6 8.9 %collective-permute-start.4 = (f32[16,256]{1,0:T(8,128)S(1)}, f32[16,256]{1,0:T(8,128)S(1)}, u32[]{:S(2)}, u32[]{:S(2)}) collective-permute-start(f32[16,256]{1,0:T(8,128)S(1)} %get-tuple-element.32), channel_id=1, source_target_pairs={{0,1},{1,2},{2,3},{3,0},{4,5},{5,6},{6,7},{7,4},{8,9},{9,10},{10,1... | collective-permute-start | bytes 49160 | tf_op jit(solution)/shard_map/ppermute | solution.py:52
  37.0 6.2 %collective-permute-start.5 = (f32[16,256]{1,0:T(8,128)S(1)}, f32[16,256]{1,0:T(8,128)S(1)}, u32[]{:S(2)}, u32[]{:S(2)}) collective-permute-start(f32[16,256]{1,0:T(8,128)S(1)} %get-tuple-element.33), channel_id=1, source_target_pairs={{1,0},{2,1},{3,2},{0,3},{5,4},{6,5},{7,6},{4,7},{9,8},{10,9},{11,1... | collective-permute-start | bytes 49160 | tf_op jit(solution)/shard_map/ppermute | solution.py:52
  53.8 60.0 %copy-start.1 = (f32[64,64,256]{2,1,0:T(8,128)S(1)}, f32[64,64,256]{2,1,0:T(8,128)}, u32[]{:S(2)}) copy-start(f32[64,64,256]{2,1,0:T(8,128)} %f_ref.5) | copy-start | bytes 12582916
  53.8 22.9 %collective-permute-start.8 = (f32[12,32,256]{2,1,0:T(8,128)S(1)}, f32[12,32,256]{2,1,0:T(8,128)S(1)}, u32[]{:S(2)}, u32[]{:S(2)}) collective-permute-start(f32[12,32,256]{2,1,0:T(8,128)S(1)} %get-tuple-element.39), channel_id=1, source_target_pairs={{0,4},{4,8},{8,12},{12,16},{16,20},{20,24},{24,28},{28,32},{32,36}... | collective-permute-start | bytes 1179656 | tf_op jit(solution)/shard_map/ppermute | solution.py:52
  53.9 22.8 %collective-permute-start.9 = (f32[12,32,256]{2,1,0:T(8,128)S(1)}, f32[12,32,256]{2,1,0:T(8,128)S(1)}, u32[]{:S(2)}, u32[]{:S(2)}) collective-permute-start(f32[12,32,256]{2,1,0:T(8,128)S(1)} %get-tuple-element.40), channel_id=1, source_target_pairs={{4,0},{8,4},{12,8},{16,12},{20,16},{24,20},{28,24},{32,28},{36,32}... | collective-permute-start | bytes 1179656 | tf_op jit(solution)/shard_map/ppermute | solution.py:52
  59.9 21.8 %collective-permute-start.6 = (f32[12,32,256]{2,1,0:T(8,128)S(1)}, f32[12,32,256]{2,1,0:T(8,128)S(1)}, u32[]{:S(2)}, u32[]{:S(2)}) collective-permute-start(f32[12,32,256]{2,1,0:T(8,128)S(1)} %get-tuple-element.37), channel_id=1, source_target_pairs={{0,1},{1,2},{2,3},{3,0},{4,5},{5,6},{6,7},{7,4},{8,9},{9,10},{10,1... | collective-permute-start | bytes 1179656 | tf_op jit(solution)/shard_map/ppermute | solution.py:52
  63.0 18.6 %collective-permute-start.7 = (f32[12,32,256]{2,1,0:T(8,128)S(1)}, f32[12,32,256]{2,1,0:T(8,128)S(1)}, u32[]{:S(2)}, u32[]{:S(2)}) collective-permute-start(f32[12,32,256]{2,1,0:T(8,128)S(1)} %get-tuple-element.38), channel_id=1, source_target_pairs={{1,0},{2,1},{3,2},{0,3},{5,4},{6,5},{7,6},{4,7},{9,8},{10,9},{11,1... | collective-permute-start | bytes 1179656 | tf_op jit(solution)/shard_map/ppermute | solution.py:52
  76.8 7.6 %collective-permute-start.10 = (f32[64,256]{1,0:T(8,128)S(1)}, f32[64,256]{1,0:T(8,128)S(1)}, u32[]{:S(2)}, u32[]{:S(2)}) collective-permute-start(f32[64,256]{1,0:T(8,128)S(1)} %get-tuple-element.41), channel_id=1, source_target_pairs={{0,1},{1,2},{2,3},{3,0},{4,5},{5,6},{6,7},{7,4},{8,9},{9,10},{10,1... | collective-permute-start | bytes 196616 | tf_op jit(solution)/shard_map/ppermute | solution.py:52
  81.4 5.9 %collective-permute-start.11 = (f32[64,256]{1,0:T(8,128)S(1)}, f32[64,256]{1,0:T(8,128)S(1)}, u32[]{:S(2)}, u32[]{:S(2)}) collective-permute-start(f32[64,256]{1,0:T(8,128)S(1)} %get-tuple-element.42), channel_id=1, source_target_pairs={{1,0},{2,1},{3,2},{0,3},{5,4},{6,5},{7,6},{4,7},{9,8},{10,9},{11,1... | collective-permute-start | bytes 196616 | tf_op jit(solution)/shard_map/ppermute | solution.py:52
  93.3 14.5 %collective-permute-start.14 = (f32[3,64,256]{2,1,0:T(8,128)S(1)}, f32[3,64,256]{2,1,0:T(8,128)S(1)}, u32[]{:S(2)}, u32[]{:S(2)}) collective-permute-start(f32[3,64,256]{2,1,0:T(8,128)S(1)} %get-tuple-element.50), channel_id=1, source_target_pairs={{0,4},{4,8},{8,12},{12,16},{16,20},{20,24},{24,28},{28,32},{32,36}... | collective-permute-start | bytes 589832 | tf_op jit(solution)/shard_map/ppermute | solution.py:52
  93.4 14.4 %collective-permute-start.15 = (f32[3,64,256]{2,1,0:T(8,128)S(1)}, f32[3,64,256]{2,1,0:T(8,128)S(1)}, u32[]{:S(2)}, u32[]{:S(2)}) collective-permute-start(f32[3,64,256]{2,1,0:T(8,128)S(1)} %get-tuple-element.51), channel_id=1, source_target_pairs={{4,0},{8,4},{12,8},{16,12},{20,16},{24,20},{28,24},{32,28},{36,32}... | collective-permute-start | bytes 589832 | tf_op jit(solution)/shard_map/ppermute | solution.py:52
  99.3 12.7 %collective-permute-start.12 = (f32[3,64,256]{2,1,0:T(8,128)S(1)}, f32[3,64,256]{2,1,0:T(8,128)S(1)}, u32[]{:S(2)}, u32[]{:S(2)}) collective-permute-start(f32[3,64,256]{2,1,0:T(8,128)S(1)} %get-tuple-element.48), channel_id=1, source_target_pairs={{0,1},{1,2},{2,3},{3,0},{4,5},{5,6},{6,7},{7,4},{8,9},{9,10},{10,1... | collective-permute-start | bytes 589832 | tf_op jit(solution)/shard_map/ppermute | solution.py:52
  100.3 11.7 %collective-permute-start.13 = (f32[3,64,256]{2,1,0:T(8,128)S(1)}, f32[3,64,256]{2,1,0:T(8,128)S(1)}, u32[]{:S(2)}, u32[]{:S(2)}) collective-permute-start(f32[3,64,256]{2,1,0:T(8,128)S(1)} %get-tuple-element.49), channel_id=1, source_target_pairs={{1,0},{2,1},{3,2},{0,3},{5,4},{6,5},{7,6},{4,7},{9,8},{10,9},{11,1... | collective-permute-start | bytes 589832 | tf_op jit(solution)/shard_map/ppermute | solution.py:52
  107.9 5.8 %collective-permute-start.16 = (f32[8,256]{1,0:T(8,128)S(1)}, f32[8,256]{1,0:T(8,128)S(1)}, u32[]{:S(2)}, u32[]{:S(2)}) collective-permute-start(f32[8,256]{1,0:T(8,128)S(1)} %get-tuple-element.52), channel_id=1, source_target_pairs={{0,1},{1,2},{2,3},{3,0},{4,5},{5,6},{6,7},{7,4},{8,9},{9,10},{10,1... | collective-permute-start | bytes 24584 | tf_op jit(solution)/shard_map/ppermute | solution.py:52
  109.3 4.5 %collective-permute-start.17 = (f32[8,256]{1,0:T(8,128)S(1)}, f32[8,256]{1,0:T(8,128)S(1)}, u32[]{:S(2)}, u32[]{:S(2)}) collective-permute-start(f32[8,256]{1,0:T(8,128)S(1)} %get-tuple-element.53), channel_id=1, source_target_pairs={{1,0},{2,1},{3,2},{0,3},{5,4},{6,5},{7,6},{4,7},{9,8},{10,9},{11,1... | collective-permute-start | bytes 24584 | tf_op jit(solution)/shard_map/ppermute | solution.py:52
where the time goes:
time: 126 us; the launch traced here: 124 us
  starting transfers between devices  45.6 us (36%)
  waiting for transfers between devices  42.4 us (34%)
  Pallas kernels  28.7 us (23%)
  local copies, waits for them, and re-layouts  6.56 us (5%)
    ppermute x18, starting transfers between devices, exchange(): return (lax.ppermute(high, axis, up), lax.ppermute(low, axis, down))  45.6 us
    ppermute x18, waiting for transfers between devices, exchange(): return (lax.ppermute(high, axis, up), lax.ppermute(low, axis, down))  42.4 us
    pallas_call x1, Pallas kernels, before(): pl.pallas_call(before_kernel, out_shape=(shape(NY, NX, NC),) + (shape(CY,...  10.6 us
    pallas_call x1, Pallas kernels, after(): pl.pallas_call(after_kernel, out_shape=(shape(NY, NX, NC),) * 2, in_specs...  10.1 us
    unnamed x8, local copies, waits for them, and re-layouts  6.56 us
    pallas_call x1, Pallas kernels, coarse(): pl.pallas_call(coarse_kernel, out_shape=(shape(CY, CX, NC),) + (shape(3,...  6 us
  transfers between devices with their start and end apart: 18, of which 11 were waited for; matrix products, arithmetic and copies ran while one was open for 0% of the time, Pallas kernels for 0%

commit v1 on v0

v1 whole, which is shorter than its diff:
```python
import jax
import jax.numpy as jnp
from jax import lax
from jax.experimental import pallas as pl
from jax.experimental.pallas import tpu as pltpu
from jax.sharding import PartitionSpec as P

NY, NX, NC = 64, 64, 256
HALVES = 2
LANES = 128
DEEP = 3
LEFT = 16
FY, FX = NY + 2 * DEEP, NX + 2 * LEFT
CY, CX = NY // 2, NX // 2
WIDE = 6
TOP = 8
GY, GX = CY + 20, CX + 2 * LEFT
BLOCK = 4

VMEM = pltpu.VMEM
F32 = jnp.float32
IN_VMEM = pl.BlockSpec(memory_space=VMEM)
IN_HBM = pl.BlockSpec(memory_space=pltpu.HBM)

SLOT = 64
U1, U2, SWEPT, F1, M1 = range(5)
ENDS = 5 * SLOT
STRIP = ENDS + 8


FINE_CELLS = tuple(
    (side, slot * SLOT, n, k, dy)
    for k, slot, n, dy in ((0, U1, 2, 1), (0, U2, 1, 2), (1, F1, 1, 1), (2, M1, 1, 1))
    for side in range(2)
)
VALUE_CELLS = tuple(c for c in FINE_CELLS if c[3] == 0)
COARSE_CELLS = tuple(
    (side, (k * WIDE + (WIDE - dy if side == 0 else dy - 1)) * CX, WIDE - dy, k, dy)
    for k in range(2)
    for side in range(2)
    for dy in range(1, WIDE)
)


def half(c):
    return pl.ds(c * LANES, LANES)


def shape(*dims):
    return jax.ShapeDtypeStruct(dims, F32)


def exchange(low, high, axis):
    size = lax.axis_size(axis)
    up = [(i, (i + 1) % size) for i in range(size)]
    down = [(b, a) for a, b in up]
    return lax.ppermute(high, axis, up), lax.ppermute(low, axis, down)


def pack_kernel(cells, width, n_lo, n_hi, down, up):
    at = 0
    for side, row, n, _, _ in cells:
        src = (n_lo, n_hi)[side]
        down[pl.ds(at, n), :] = src[pl.ds(row, n), :]
        up[pl.ds(at, n), :] = src[pl.ds(row + width - n, n), :]
        at += n


def pack(cells, width, n_lo, n_hi):
    size = -(-sum(c[2] for c in cells) // 8) * 8
    return pl.pallas_call(
        lambda *refs: pack_kernel(cells, width, *refs),
        out_shape=(shape(size, NC),) * 2,
        in_specs=[IN_VMEM] * 2,
        out_specs=(IN_VMEM,) * 2,
        compiler_params=pltpu.CompilerParams(vmem_limit_bytes=7 * 2**20),
        name="pack",
    )(n_lo, n_hi)


def halos(cells, width, east_low, east_high, north_low, north_high):
    e_lo, e_hi = exchange(east_low, east_high, "east")
    n_lo, n_hi = exchange(north_low, north_high, "north")
    down, up = pack(cells, width, n_lo, n_hi)
    c_lo, c_hi = exchange(down, up, "east")
    return e_lo, e_hi, n_lo, n_hi, c_lo, c_hi


def weight_of(mass):
    return 0.8 / (4.0 + mass)


def swept_line(u1, u2, u3, f2, m2, line):
    line[pl.ds(8, SLOT), :] = u2
    s = (u1 + u3) + (line[pl.ds(7, SLOT), :] + line[pl.ds(9, SLOT), :]) + f2
    return 0.2 * u2 + weight_of(m2) * s


def clear_ends(line):
    line[pl.ds(0, 8), :] = jnp.zeros((8, LANES), F32)
    line[pl.ds(8 + SLOT, 8), :] = jnp.zeros((8, LANES), F32)


def write_strip(get, out, keep, line, h):
    u1, u2, u3, f2, m2 = get(0, 1), get(0, 2), get(0, 3), get(1, 2), get(2, 2)
    out[pl.ds(U1 * SLOT, SLOT), h] = u1
    out[pl.ds(U2 * SLOT, SLOT), h] = u2
    out[pl.ds(SWEPT * SLOT, SLOT), h] = swept_line(u1, u2, u3, f2, m2, line)
    out[pl.ds(F1 * SLOT, SLOT), h] = get(1, 1)
    out[pl.ds(M1 * SLOT, SLOT), h] = get(2, 1)
    keep[pl.ds(0, SLOT), h] = f2
    keep[pl.ds(SLOT, SLOT), h] = m2
    out[pl.ds(ENDS, 1), h] = keep[pl.ds(SLOT, 1), h]
    out[pl.ds(ENDS + 1, 1), h] = keep[pl.ds(2 * SLOT - 1, 1), h]
    out[pl.ds(ENDS + 2, 6), h] = jnp.zeros((6, LANES), F32)


def north_edges_kernel(u_ref, f_ref, m_ref, nl, nh, knl, knh, lines, line, sems):
    copies = []
    for side in range(2):
        for k, ref in enumerate((u_ref, f_ref, m_ref)):
            copy = pltpu.make_async_copy(
                ref.at[pl.ds(side * (NY - 3), 3)], lines.at[k, side], sems.at[k, side]
            )
            copy.start()
            copies.append(copy)
    clear_ends(line)
    for copy in copies:
        copy.wait()
    for side in range(2):
        for c in range(HALVES):
            h = half(c)
            write_strip(
                lambda k, d: lines[k, side, d - 1 if side == 0 else 3 - d, :, h],
                (nl, nh)[side], (knl, knh)[side], line, h,
            )


def east_edges_kernel(u_ref, f_ref, m_ref, el, eh, kel, keh, tiles, line, sems):
    copies = []
    for side in range(2):
        for c in range(HALVES):
            for k, ref in enumerate((u_ref, f_ref, m_ref)):
                copy = pltpu.make_async_copy(
                    ref.at[:, pl.ds(side * (NX - 8), 8), half(c)],
                    tiles.at[k, side, c],
                    sems.at[k, side, c],
                )
                copy.start()
                copies.append(copy)
    clear_ends(line)
    for copy in copies:
        copy.wait()
    for side in range(2):
        for c in range(HALVES):

            def get(k, d):
                flat = tiles.at[k, side, c].reshape(NY * 8, LANES)
                return flat[pl.ds(d - 1 if side == 0 else 8 - d, NY, stride=8), :]

            write_strip(get, (el, eh)[side], (kel, keh)[side], line, half(c))


def edges(kernel, buffer, sems, u, f, m):
    return pl.pallas_call(
        kernel,
        out_shape=(shape(STRIP, NC),) * 2 + (shape(2 * SLOT, NC),) * 2,
        in_specs=[IN_HBM] * 3,
        out_specs=(IN_VMEM,) * 4,
        scratch_shapes=[
            VMEM(buffer, F32),
            VMEM((SLOT + 16, LANES), F32),
            pltpu.SemaphoreType.DMA(sems),
        ],
        compiler_params=pltpu.CompilerParams(vmem_limit_bytes=58 * 2**20),
    )(u, f, m)


def mass_kernel(m_ref, low, high, tiles, pair, sems):
    copies = []
    for side in range(2):
        for c in range(HALVES):
            copy = pltpu.make_async_copy(
                m_ref.at[:, pl.ds(side * (NX - 16), 16), half(c)], tiles.at[side, c], sems.at[side, c]
            )
            copy.start()
            copies.append(copy)
    for side in range(2):
        for c in range(HALVES):
            copies[side * HALVES + c].wait()
            flat = tiles.at[side, c].reshape(NY * 16, LANES)
            for d in range(WIDE):
                x = 2 * d + (0 if side == 0 else 16 - 2 * WIDE)
                pair[...] = flat[pl.ds(x, NY, stride=16), :] + flat[pl.ds(x + 1, NY, stride=16), :]
                (low, high)[side][pl.ds(d * CY, CY), half(c)] = 0.5 * (
                    pair[pl.ds(0, CY, stride=2), :] + pair[pl.ds(1, CY, stride=2), :]
                )


def mass_columns(m):
    return pl.pallas_call(
        mass_kernel,
        out_shape=(shape(WIDE * CY, NC),) * 2,
        in_specs=[IN_HBM],
        out_specs=(IN_VMEM,) * 2,
        scratch_shapes=[
            VMEM((2, HALVES, NY, 16, LANES), F32),
            VMEM((NY, LANES), F32),
            pltpu.SemaphoreType.DMA((2, HALVES)),
        ],
        compiler_params=pltpu.CompilerParams(vmem_limit_bytes=16 * 2**20),
        name="mass_columns",
    )(m)


def place_corners(dst, h, sizes, array, cells, c_lo, c_hi, of=lambda x: x):
    top, ny, nx, _ = sizes
    where = 0
    for side, _, n, k, dy in cells:
        if k == array:
            row = top - dy if side == 0 else top + ny + dy - 1
            dst[row, pl.ds(LEFT - n, n), :] = of(c_lo[pl.ds(where, n), h])
            dst[row, pl.ds(LEFT + nx, n), :] = of(c_hi[pl.ds(where, n), h])
        where += n


def place_lines(dst, h, depth, slot, e_lo, e_hi, n_lo, n_hi, of=lambda x: x):
    flat = dst.reshape(FY * FX, LANES)
    at = pl.ds(slot * SLOT, SLOT)
    dst[DEEP - depth, pl.ds(LEFT, NX), :] = of(n_lo[at, h])
    dst[DEEP + NY + depth - 1, pl.ds(LEFT, NX), :] = of(n_hi[at, h])
    flat[pl.ds(DEEP * FX + LEFT - depth, NY, stride=FX), :] = of(e_lo[at, h])
    flat[pl.ds(DEEP * FX + LEFT + NX + depth - 1, NY, stride=FX), :] = of(e_hi[at, h])


FINE = (DEEP, NY, NX, FX)


def stencil(src, r, col, count, height):
    last = lax.broadcasted_iota(jnp.int32, (8, LANES), 0) == 7
    cache = {}

    def tile(k, t):
        if (k, t) not in cache:
            cache[k, t] = src[r + k, pl.ds(col + 8 * t, 8), :]
        return cache[k, t]

    turn = [pltpu.roll(tile(k, 0), 7, 0) for k in range(height)]
    for t in range(count):
        for k in range(height):
            following = pltpu.roll(tile(k, t + 1), 7, 0)
            right = jnp.where(last, following, turn[k])
            turn[k] = following
            left = src[r + k, pl.ds(col + 8 * t - 1, 8), :]
            yield k, t, tile(k, t), (tile(k - 1, t) + tile(k + 1, t)) + (left + right)


def sweep_rows(src, dst, load, weight, start, rows, col, count, mass=None):
    def block(i, carry):
        r = start + BLOCK * i
        for k, t, mid, s in stencil(src, r, col, count, BLOCK):
            at = pl.ds(col + 8 * t, 8)
            if mass is None:
                w = weight[r + k, at, :]
            else:
                w = 0.8 / (4.0 + mass[r + k, at, :])
                weight[r + k, at, :] = w
            dst[r + k, at, :] = 0.2 * mid + w * (s + load[r + k, at, :])
        return carry

    lax.fori_loop(0, rows // BLOCK, block, 0)


def two_sweeps(u, vs, f, ws, h, strips, ends, mass=None):
    args = (1, NY + 4, LEFT - 8, NX // 8 + 2)
    sweep_rows(u, vs, f, ws, *args, mass=mass)
    place_lines(vs, h, 2, SWEPT, *strips)
    low, high = DEEP, DEEP + NY - 1
    left, right = LEFT, LEFT + NX - 1
    e_lo, e_hi, n_lo, n_hi = ends

    def complete(row, col, from_row, from_col, mass):
        vs[row, pl.ds(col, 1), :] = (
            vs[row, pl.ds(col, 1), :] + weight_of(mass) * u[from_row, pl.ds(from_col, 1), :]
        )

    first, last = pl.ds(ENDS, 1), pl.ds(ENDS + 1, 1)
    for col, strip in ((left - 2, e_lo), (right + 2, e_hi)):
        complete(low, col, low - 1, col, strip[first, h])
        complete(high, col, high + 1, col, strip[last, h])
    for row, strip in ((low - 2, n_lo), (high + 2, n_hi)):
        complete(row, left, row, left - 1, strip[first, h])
        complete(row, right, row, right + 1, strip[last, h])
    sweep_rows(vs, u, f, ws, *args)


PADDED = (HALVES, FY, FX, LANES)


def load_kernel(u_ref, f_ref, m_ref, us, fs, ms, ws, sems):
    copies = {}
    for k, (ref, dst) in reversed(list(enumerate(((u_ref, us), (f_ref, fs), (m_ref, ms))))):
        for c in range(HALVES):
            copies[k, c] = pltpu.make_async_copy(
                ref.at[:, :, half(c)],
                dst.at[c, pl.ds(DEEP, NY), pl.ds(LEFT, NX), :],
                sems.at[k, c],
            )
            copies[k, c].start()
    for c in range(HALVES):
        copies[2, c].wait()

        def rows(i, carry):
            for k in range(BLOCK):
                at = (c, DEEP + BLOCK * i + k, pl.ds(LEFT, NX), slice(None))
                ws[at] = weight_of(ms[at])
            return carry

        lax.fori_loop(0, NY // BLOCK, rows, 0)
    for k in range(2):
        for c in range(HALVES):
            copies[k, c].wait()


def load(u, f, m):
    return pl.pallas_call(
        load_kernel,
        out_shape=(shape(*PADDED),) * 4,
        in_specs=[IN_HBM] * 3,
        out_specs=(IN_VMEM,) * 4,
        scratch_shapes=[pltpu.SemaphoreType.DMA((3, HALVES))],
        compiler_params=pltpu.CompilerParams(vmem_limit_bytes=7 * 2**20),
        cost_estimate=pl.CostEstimate(flops=2**26, bytes_accessed=12 * 2**20, transcendentals=0),
        name="load",
    )(u, f, m)


def before_kernel(
    _u, _f, _m, _w, e_lo, e_hi, n_lo, n_hi, c_lo, c_hi,
    us, fs, ms, ws, u2_ref, cl_ref, cm_ref, cel, ceh, cnl, cnh, uel, ueh, unl, unh,
    vs, pair,
):
    strips = (e_lo, e_hi, n_lo, n_hi)
    for c in range(HALVES):
        h = half(c)
        u, f, m, w = us.at[c], fs.at[c], ms.at[c], ws.at[c]
        for dst, depth, slot in ((u, 1, U1), (u, 2, U2), (f, 1, F1), (m, 1, M1)):
            place_lines(dst, h, depth, slot, *strips)
        place_lines(w, h, 1, M1, *strips, of=weight_of)
        for k, dst in enumerate((u, f, m)):
            place_corners(dst, h, FINE, k, FINE_CELLS, c_lo, c_hi)
        place_corners(w, h, FINE, 2, FINE_CELLS, c_lo, c_hi, of=weight_of)
        two_sweeps(u, vs, f, w, h, strips, strips)

        def coarse_rows(i, carry):
            r = DEEP + 4 * i
            sums = {}
            for k, t, mid, s in stencil(u, r, LEFT, NX // 8, 4):
                at = pl.ds(LEFT + 8 * t, 8)
                mass = m[r + k, at, :]
                u2_ref[4 * i + k, pl.ds(8 * t, 8), h] = mid
                d = f[r + k, at, :] + s - (4.0 + mass) * mid
                if k % 2 == 0:
                    sums[t] = (d, mass)
                else:
                    pair[k // 2, 0, pl.ds(8 * t, 8), :] = sums[t][0] + d
                    pair[k // 2, 1, pl.ds(8 * t, 8), :] = sums[t][1] + mass
            for k in range(2):
                for which, ref in enumerate((cl_ref, cm_ref)):
                    ref[2 * i + k, :, h] = 0.5 * (
                        pair[k, which, pl.ds(0, CX, stride=2), :]
                        + pair[k, which, pl.ds(1, CX, stride=2), :]
                    )
            return carry

        lax.fori_loop(0, NY // 4, coarse_rows, 0)
        flat = u.reshape(FY * FX, LANES)
        for d in range(3):
            at = pl.ds(d * SLOT, SLOT)
            uel[at, h] = flat[pl.ds(DEEP * FX + LEFT + d, NY, stride=FX), :]
            ueh[at, h] = flat[pl.ds(DEEP * FX + LEFT + NX - 1 - d, NY, stride=FX), :]
            unl[at, h] = u[DEEP + d, pl.ds(LEFT, NX), :]
            unh[at, h] = u[DEEP + NY - 1 - d, pl.ds(LEFT, NX), :]
    for d in range(WIDE):
        cel[pl.ds(d * CY, CY), :] = cl_ref[:, d, :]
        ceh[pl.ds(d * CY, CY), :] = cl_ref[:, CX - WIDE + d, :]
        for k, ref in enumerate((cl_ref, cm_ref)):
            at = pl.ds((k * WIDE + d) * CX, CX)
            cnl[at, :] = ref[d]
            cnh[at, :] = ref[CY - WIDE + d]


def before(padded, strips):
    return pl.pallas_call(
        before_kernel,
        out_shape=(shape(*PADDED),) * 4
        + (shape(NY, NX, NC),)
        + (shape(CY, CX, NC),) * 2
        + (shape(WIDE * CY, NC),) * 2
        + (shape(2 * WIDE * CX, NC),) * 2
        + (shape(3 * SLOT, NC),) * 4,
        in_specs=[IN_VMEM] * 10,
        out_specs=(IN_VMEM,) * 15,
        input_output_aliases={k: k for k in range(4)},
        scratch_shapes=[VMEM((FY, FX, LANES), F32), VMEM((2, 2, NX, LANES), F32)],
        compiler_params=pltpu.CompilerParams(vmem_limit_bytes=7 * 2**20),
        name="before",
    )(*padded, *strips)


def coarse_kernel(
    cl_ref, cm_ref, me_lo, me_hi, e_lo, e_hi, n_lo, n_hi, c_lo, c_hi,
    uel, ueh, unl, unh, kel, keh, knl, knh,
    e_ref, ael, aeh, anl, anh,
    ls, ws, es, gs, tmp, line,
):
    rows, cols = pl.ds(TOP, CY), pl.ds(LEFT, CX)
    clear_ends(line)
    for c in range(HALVES):
        h = half(c)
        for k, (dst, ref, lo, hi) in enumerate(
            ((ls, cl_ref, e_lo, e_hi), (ws, cm_ref, me_lo, me_hi))
        ):
            dst[rows, cols, :] = ref[:, :, h]
            flat = dst.reshape(GY * GX, LANES)
            for d in range(WIDE):
                at = pl.ds((k * WIDE + d) * CX, CX)
                dst[TOP - WIDE + d, cols, :] = n_lo[at, h]
                dst[TOP + CY + d, cols, :] = n_hi[at, h]
                at = pl.ds(d * CY, CY)
                flat[pl.ds(TOP * GX + LEFT - WIDE + d, CY, stride=GX), :] = lo[at, h]
                flat[pl.ds(TOP * GX + LEFT + CX + d, CY, stride=GX), :] = hi[at, h]
            place_corners(dst, h, (TOP, CY, CX, GX), k, COARSE_CELLS, c_lo, c_hi)
        wide = pl.ds(LEFT - 8, CX + 16)

        def first(i, carry):
            for k in range(BLOCK):
                r = TOP - WIDE + BLOCK * i + k
                w = 0.8 / (4.0 + ws[r, wide, :])
                ws[r, wide, :] = w
                es[r, wide, :] = w * ls[r, wide, :]
            return carry

        lax.fori_loop(0, (CY + 2 * WIDE) // BLOCK, first, 0)
        src, dst = es, gs
        for sweep in range(6):
            ring = 5 - sweep
            count = -(-(CY + 2 * ring) // BLOCK) * BLOCK
            sweep_rows(src, dst, ls, ws, TOP - ring, count, LEFT - 8, CX // 8 + 2)
            src, dst = dst, src
        e_ref[:, :, h] = src[rows, cols, :]
        flat = src.reshape(GY * GX, LANES)

        def spread(line):
            tmp[pl.ds(0, CX, stride=2), :] = line
            tmp[pl.ds(1, CX, stride=2), :] = line
            return tmp[...]

        for out, old, keep, where, high in (
            (ael, uel, kel, "x", False), (aeh, ueh, keh, "x", True),
            (anl, unl, knl, "y", False), (anh, unh, knh, "y", True),
        ):
            values = []
            for d in range(3):
                at = (CX - 1 - d // 2) if high else d // 2
                if where == "x":
                    coarse_line = flat[pl.ds(TOP * GX + LEFT + at, CY, stride=GX), :]
                else:
                    coarse_line = src[TOP + at, cols, :]
                values.append(old[pl.ds(d * SLOT, SLOT), h] + spread(coarse_line))
            f2, m2 = keep[pl.ds(0, SLOT), h], keep[pl.ds(SLOT, SLOT), h]
            out[pl.ds(U1 * SLOT, SLOT), h] = values[0]
            out[pl.ds(U2 * SLOT, SLOT), h] = values[1]
            out[pl.ds(SWEPT * SLOT, SLOT), h] = swept_line(*values, f2, m2, line)


def coarse(right, mass, mass_strips, strips, u_strips, kept):
    return pl.pallas_call(
        coarse_kernel,
        out_shape=(shape(CY, CX, NC),) + (shape(3 * SLOT, NC),) * 4,
        in_specs=[IN_VMEM] * 18,
        out_specs=(IN_VMEM,) * 5,
        scratch_shapes=[VMEM((GY, GX, LANES), F32)] * 4
        + [VMEM((NY, LANES), F32), VMEM((SLOT + 16, LANES), F32)],
        compiler_params=pltpu.CompilerParams(vmem_limit_bytes=7 * 2**20),
        name="coarse",
    )(right, mass, *mass_strips, *strips, *u_strips, *kept)


def fetch(refs, dsts, sems):
    copies = []
    for c in range(HALVES):
        copies.append([])
        for k, (ref, dst) in enumerate(zip(refs, dsts)):
            copy = pltpu.make_async_copy(
                ref.at[:, :, half(c)],
                dst.at[c, pl.ds(DEEP, NY), pl.ds(LEFT, NX), :],
                sems.at[c, k],
            )
            copy.start()
            copies[c].append(copy)
    return copies


def fine_scratch():
    both = VMEM((HALVES, FY, FX, LANES), F32)
    return [both] * 3 + [VMEM((FY, FX, LANES), F32)] * 2


def after_kernel(
    u_ref, f_ref, m_ref, e_ref, e_lo, e_hi, n_lo, n_hi, c_lo, c_hi,
    h_el, h_eh, h_nl, h_nh, h_cl, h_ch,
    out_ref, rest_ref,
    us, fs, ms, ws, vs, tmp, sems, out_sems,
):
    copies = fetch((u_ref, f_ref, m_ref), (us, fs, ms), sems)
    strips, old = (e_lo, e_hi, n_lo, n_hi), (h_el, h_eh, h_nl, h_nh)
    outs = []
    for c in range(HALVES):
        h = half(c)
        u, f, m = us.at[c], fs.at[c], ms.at[c]
        mid = pl.ds(LEFT, NX)
        place_lines(u, h, 1, U1, *strips)
        place_lines(u, h, 2, U2, *strips)
        place_corners(u, h, FINE, 0, VALUE_CELLS, c_lo, c_hi)
        for k, dst, slot in ((1, f, F1), (2, m, M1)):
            place_lines(dst, h, 1, slot, *old)
            place_corners(dst, h, FINE, k, FINE_CELLS, h_cl, h_ch)
        for copy in copies[c]:
            copy.wait()

        def add(i, carry):
            for k in range(4):
                line = e_ref[4 * i + k, :, h]
                tmp[k, pl.ds(0, CX, stride=2), :] = line
                tmp[k, pl.ds(1, CX, stride=2), :] = line
            for k in range(4):
                t = tmp[k]
                for j in range(2):
                    r = DEEP + 8 * i + 2 * k + j
                    u[r, mid, :] = u[r, mid, :] + t
            return carry

        lax.fori_loop(0, CY // 4, add, 0)
        two_sweeps(u, vs, f, ws, h, strips, old, mass=m)
        block = (pl.ds(DEEP, NY), mid)
        out = pltpu.make_async_copy(
            u.at[block[0], block[1], :], out_ref.at[:, :, h], out_sems.at[c, 0]
        )
        out.start()
        outs.append(out)

        def rest(i, carry):
            r = DEEP + BLOCK * i
            for k, t, value, s in stencil(u, r, LEFT, NX // 8, BLOCK):
                at = pl.ds(LEFT + 8 * t, 8)
                f[r + k, at, :] = f[r + k, at, :] + s - (4.0 + m[r + k, at, :]) * value
            return carry

        lax.fori_loop(0, NY // BLOCK, rest, 0)
        out = pltpu.make_async_copy(
            f.at[block[0], block[1], :], rest_ref.at[:, :, h], out_sems.at[c, 1]
        )
        out.start()
        outs.append(out)
    for out in outs:
        out.wait()


def after(u, f, m, e, strips, old):
    return pl.pallas_call(
        after_kernel,
        out_shape=(shape(NY, NX, NC),) * 2,
        in_specs=[IN_HBM] * 3 + [IN_VMEM] * 13,
        out_specs=(IN_HBM,) * 2,
        scratch_shapes=fine_scratch()
        + [
            VMEM((4, NX, LANES), F32),
            pltpu.SemaphoreType.DMA((HALVES, 3)),
            pltpu.SemaphoreType.DMA((HALVES, 2)),
        ],
        compiler_params=pltpu.CompilerParams(vmem_limit_bytes=40 * 2**20),
        name="after",
    )(u, f, m, e, *strips, *old)


def body(right_side, first_guess, mass_term):
    f, u, m = right_side, first_guess, mass_term
    nl, nh, *north_kept = edges(north_edges_kernel, (3, 2, 3, NX, NC), (3, 2), u, f, m)
    el, eh, *kept = edges(east_edges_kernel, (3, 2, HALVES, NY, 8, LANES), (3, 2, HALVES), u, f, m)
    kept += north_kept
    old = halos(FINE_CELLS, NX, el, eh, nl, nh)
    columns = mass_columns(m)
    padded = load(u, f, m)
    mass_strips = exchange(*columns, "east")
    _, _, _, _, u2, right, mass, cel, ceh, cnl, cnh, *u_strips = before(padded, old)
    wide = halos(COARSE_CELLS, CX, cel, ceh, cnl, cnh)
    e, *edge_values = coarse(right, mass, mass_strips, wide, u_strips, kept)
    strips = halos(VALUE_CELLS, NX, *edge_values)
    return after(u2, f, m, e, strips, old)


def solution(mesh):
    spec = P("north", "east", None)
    return jax.shard_map(
        body, mesh=mesh, in_specs=(spec,) * 3, out_specs=(spec, spec), check_vma=False
    )
```

time: 126 us -> 132 us (1.048)
  the two profiles are of different devices: /device:TPU:0 before, /device:TPU:32 now
where the time goes in v1:
time: 132 us
  starting transfers between devices  56.4 us (43%)
  Pallas kernels  31.3 us (24%)
  local copies, waits for them, and re-layouts  21.7 us (16%)
  waiting for transfers between devices  21.3 us (16%)
    ppermute x20, starting transfers between devices, exchange(): return (lax.ppermute(high, axis, up), lax.ppermute(low, axis, down))  56.4 us
    unnamed x28, local copies, waits for them, and re-layouts  21.7 us
    ppermute x20, waiting for transfers between devices, exchange(): return (lax.ppermute(high, axis, up), lax.ppermute(low, axis, down))  21.3 us
    pallas_call x1, Pallas kernels, after(): pl.pallas_call(after_kernel, out_shape=(shape(NY, NX, NC),) * 2, in_specs...  10.1 us
    pallas_call x1, Pallas kernels, before(): pl.pallas_call(before_kernel, out_shape=(shape(*PADDED),) * 4 + (shape(NY...  7.08 us
    pallas_call x1, Pallas kernels, coarse(): pl.pallas_call(coarse_kernel, out_shape=(shape(CY, CX, NC),) + (shape(3 *...  6.11 us
    pallas_call x2, Pallas kernels, edges(): pl.pallas_call(kernel, out_shape=(shape(STRIP, NC),) * 2 + (shape(2 * SLO...  5.38 us
  transfers between devices with their start and end apart: 20, of which 6 were waited for; matrix products, arithmetic and copies ran while one was open for 0% of the time, Pallas kernels for 4%

profile of v1, /device:TPU:32, one launch (start us, length us, event | category | flops | bytes accessed | tf_op | source)
XLA Modules:
  0.0 131.7 jit_solution(6179334726716981627)
XLA Ops:
  0.6 2.4 %shard_map.51 = (f32[328,256]{1,0:T(8,128)}, f32[328,256]{1,0:T(8,128)}, f32[128,256]{1,0:T(8,128)}, f32[128,256]{1,0:T(8,128)}) custom-call(f32[64,64,256]{2,1,0:T(8,128)} %u_ref.5, f32[64,64,256]{2,1,0:T(8,128)} %f_ref.7, f32[64,64,256]{2,1,0:T(8,128)} %m_ref.9), custom_call_target="tpu_custom_call" | custom-call | tf_op jit(solution)/shard_map/pallas_call | solution.py:165
  3.1 6.0 %collective-permute-start.3 = (f32[328,256]{1,0:T(8,128)}, f32[328,256]{1,0:T(8,128)S(1)}, u32[]{:S(2)}, u32[]{:S(2)}) collective-permute-start(f32[328,256]{1,0:T(8,128)} %get-tuple-element.45), channel_id=1, source_target_pairs={{4,0},{8,4},{12,8},{16,12},{20,16},{24,20},{28,24},{32,28},{36,32}... | collective-permute-start | bytes 1007624 | tf_op jit(solution)/shard_map/ppermute | solution.py:57
  9.1 3.0 %shard_map.50 = (f32[328,256]{1,0:T(8,128)}, f32[328,256]{1,0:T(8,128)}, f32[128,256]{1,0:T(8,128)}, f32[128,256]{1,0:T(8,128)}) custom-call(f32[64,64,256]{2,1,0:T(8,128)} %u_ref.5, f32[64,64,256]{2,1,0:T(8,128)} %f_ref.7, f32[64,64,256]{2,1,0:T(8,128)} %m_ref.9), custom_call_target="tpu_custom_call" | custom-call | tf_op jit(solution)/shard_map/pallas_call | solution.py:165
  12.1 3.3 %collective-permute-start = (f32[328,256]{1,0:T(8,128)}, f32[328,256]{1,0:T(8,128)S(1)}, u32[]{:S(2)}, u32[]{:S(2)}) collective-permute-start(f32[328,256]{1,0:T(8,128)} %get-tuple-element.42), channel_id=1, source_target_pairs={{0,1},{1,2},{2,3},{3,0},{4,5},{5,6},{6,7},{7,4},{8,9},{9,10},{10,1... | collective-permute-start | bytes 1007624 | tf_op jit(solution)/shard_map/ppermute | solution.py:57
  15.4 2.2 %collective-permute-start.1 = (f32[328,256]{1,0:T(8,128)}, f32[328,256]{1,0:T(8,128)S(1)}, u32[]{:S(2)}, u32[]{:S(2)}) collective-permute-start(f32[328,256]{1,0:T(8,128)} %get-tuple-element.43), channel_id=1, source_target_pairs={{1,0},{2,1},{3,2},{0,3},{5,4},{6,5},{7,6},{4,7},{9,8},{10,9},{11,1... | collective-permute-start | bytes 1007624 | tf_op jit(solution)/shard_map/ppermute | solution.py:57
  17.7 5.8 %collective-permute-start.4 = (f32[16,256]{1,0:T(8,128)S(1)}, f32[16,256]{1,0:T(8,128)S(1)}, u32[]{:S(2)}, u32[]{:S(2)}) collective-permute-start(f32[16,256]{1,0:T(8,128)S(1)} %get-tuple-element.46), channel_id=1, source_target_pairs={{0,1},{1,2},{2,3},{3,0},{4,5},{5,6},{6,7},{7,4},{8,9},{9,10},{10,1... | collective-permute-start | bytes 49160 | tf_op jit(solution)/shard_map/ppermute | solution.py:57
  23.5 6.8 %collective-permute-start.5 = (f32[16,256]{1,0:T(8,128)S(1)}, f32[16,256]{1,0:T(8,128)S(1)}, u32[]{:S(2)}, u32[]{:S(2)}) collective-permute-start(f32[16,256]{1,0:T(8,128)S(1)} %get-tuple-element.47), channel_id=1, source_target_pairs={{1,0},{2,1},{3,2},{0,3},{5,4},{6,5},{7,6},{4,7},{9,8},{10,9},{11,1... | collective-permute-start | bytes 49160 | tf_op jit(solution)/shard_map/ppermute | solution.py:57
  30.2 2.2 %copy-done.1 = f32[64,64,256]{2,1,0:T(8,128)S(1)} copy-done((f32[64,64,256]{2,1,0:T(8,128)S(1)}, f32[64,64,256]{2,1,0:T(8,128)}, u32[]{:S(2)}) %copy-start.1) | copy-done | bytes 4194328
  32.4 2.2 %copy-done.3 = f32[64,64,256]{2,1,0:T(8,128)S(1)} copy-done((f32[64,64,256]{2,1,0:T(8,128)S(1)}, f32[64,64,256]{2,1,0:T(8,128)}, u32[]{:S(2)}) %copy-start.3) | copy-done | bytes 4194328
  34.6 1.7 %load.1 = (f32[2,70,96,128]{3,2,1,0:T(8,128)S(1)}, f32[2,70,96,128]{3,2,1,0:T(8,128)S(1)}, f32[2,70,96,128]{3,2,1,0:T(8,128)S(1)}, f32[2,70,96,128]{3,2,1,0:T(8,128)S(1)}) custom-call(f32[64,64,256]{2,1,0:T(8,128)S(1)} %copy-done.3, f32[64,64,256]{2,1,0:T(8,128)S(1)} %copy-done.1, f32[64,64,256]{2,1,0:T(8,128)S(1)} %copy-done), custom_call_target="tpu_custom_call" | custom-call | flops 67108864 | bytes 12582912 | tf_op jit(solution)/shard_map/load/pallas_call | solution.py:326
  36.4 2.8 %copy-done.4 = f32[2,70,96,128]{3,2,1,0:T(8,128)} copy-done((f32[2,70,96,128]{3,2,1,0:T(8,128)}, f32[2,70,96,128]{3,2,1,0:T(8,128)S(1)}, u32[]{:S(2)}) %copy-start.4) | copy-done | bytes 6881304
  39.2 2.9 %copy-done.6 = f32[2,70,96,128]{3,2,1,0:T(8,128)} copy-done((f32[2,70,96,128]{3,2,1,0:T(8,128)}, f32[2,70,96,128]{3,2,1,0:T(8,128)S(1)}, u32[]{:S(2)}) %copy-start.6) | copy-done | bytes 6881304
  42.1 2.7 %copy-done.8 = f32[2,70,96,128]{3,2,1,0:T(8,128)} copy-done((f32[2,70,96,128]{3,2,1,0:T(8,128)}, f32[2,70,96,128]{3,2,1,0:T(8,128)S(1)}, u32[]{:S(2)}) %copy-start.8) | copy-done | bytes 6881304
  44.8 2.9 %copy-done.5 = f32[2,70,96,128]{3,2,1,0:T(8,128)S(1)} copy-done((f32[2,70,96,128]{3,2,1,0:T(8,128)S(1)}, f32[2,70,96,128]{3,2,1,0:T(8,128)}, u32[]{:S(2)}) %copy-start.5) | copy-done | bytes 6881304
  47.8 3.0 %copy-done.7 = f32[2,70,96,128]{3,2,1,0:T(8,128)S(1)} copy-done((f32[2,70,96,128]{3,2,1,0:T(8,128)S(1)}, f32[2,70,96,128]{3,2,1,0:T(8,128)}, u32[]{:S(2)}) %copy-start.7) | copy-done | bytes 6881304
  50.7 3.0 %copy-done.9 = f32[2,70,96,128]{3,2,1,0:T(8,128)S(1)} copy-done((f32[2,70,96,128]{3,2,1,0:T(8,128)S(1)}, f32[2,70,96,128]{3,2,1,0:T(8,128)}, u32[]{:S(2)}) %copy-start.9) | copy-done | bytes 6881304
  53.7 7.1 %before.1 = (f32[2,70,96,128]{3,2,1,0:T(8,128)S(1)}, f32[2,70,96,128]{3,2,1,0:T(8,128)S(1)}, f32[2,70,96,128]{3,2,1,0:T(8,128)S(1)}, f32[2,70,96,128]{3,2,1,0:T(...) custom-call(f32[2,70,96,128]{3,2,1,0:T(8,128)S(1)} %get-tuple-elemen, ...), custom_call_target="tpu_custom_call", output_to_operand_aliasing={{0}: (0, {}), {1}: (1, {}), {2}: (2, {}), {3}: (3, {})} | custom-call | tf_op jit(solution)/shard_map/before/pallas_call | solution.py:394
  60.9 6.0 %collective-permute-start.11 = (f32[384,256]{1,0:T(8,128)S(1)}, f32[384,256]{1,0:T(8,128)S(1)}, u32[]{:S(2)}, u32[]{:S(2)}) collective-permute-start(f32[384,256]{1,0:T(8,128)S(1)} %get-tuple-element.56), channel_id=1, source_target_pairs={{4,0},{8,4},{12,8},{16,12},{20,16},{24,20},{28,24},{32,28},{36,32}... | collective-permute-start | bytes 1179656 | tf_op jit(solution)/shard_map/ppermute | solution.py:57
  68.5 3.4 %collective-permute-start.7 = (f32[192,256]{1,0:T(8,128)S(1)}, f32[192,256]{1,0:T(8,128)S(1)}, u32[]{:S(2)}, u32[]{:S(2)}) collective-permute-start(f32[192,256]{1,0:T(8,128)S(1)} %get-tuple-element.52), channel_id=1, source_target_pairs={{1,0},{2,1},{3,2},{0,3},{5,4},{6,5},{7,6},{4,7},{9,8},{10,9},{11,1... | collective-permute-start | bytes 589832 | tf_op jit(solution)/shard_map/ppermute | solution.py:57
  72.7 10.7 %collective-permute-done.10.refs_0_.n_lo = f32[384,256]{1,0:T(8,128)S(1)} collective-permute-done((f32[384,256]{1,0:T(8,128)S(1)}, f32[384,256]{1,0:T(8,128)S(1)}, u32[]{:S(2)}, u32[]{:S(2)}) %collective-permute-start.10) | collective-permute-done | bytes 393248 | tf_op jit(solution)/shard_map/ppermute | solution.py:57
  83.4 2.5 %collective-permute-start.9 = (f32[192,256]{1,0:T(8,128)S(1)}, f32[192,256]{1,0:T(8,128)S(1)}, u32[]{:S(2)}, u32[]{:S(2)}) collective-permute-start(f32[192,256]{1,0:T(8,128)S(1)} %get-tuple-element.54), channel_id=1, source_target_pairs={{1,0},{2,1},{3,2},{0,3},{5,4},{6,5},{7,6},{4,7},{9,8},{10,9},{11,1... | collective-permute-start | bytes 589832 | tf_op jit(solution)/shard_map/ppermute | solution.py:57
  86.5 3.7 %collective-permute-start.13 = (f32[64,256]{1,0:T(8,128)S(1)}, f32[64,256]{1,0:T(8,128)S(1)}, u32[]{:S(2)}, u32[]{:S(2)}) collective-permute-start(f32[64,256]{1,0:T(8,128)S(1)} %get-tuple-element.58), channel_id=1, source_target_pairs={{1,0},{2,1},{3,2},{0,3},{5,4},{6,5},{7,6},{4,7},{9,8},{10,9},{11,1... | collective-permute-start | bytes 196616 | tf_op jit(solution)/shard_map/ppermute | solution.py:57
  90.4 2.0 %collective-permute-done.12.c_lo = f32[64,256]{1,0:T(8,128)S(1)} collective-permute-done((f32[64,256]{1,0:T(8,128)S(1)}, f32[64,256]{1,0:T(8,128)S(1)}, u32[]{:S(2)}, u32[]{:S(2)}) %collective-permute-start.12) | collective-permute-done | bytes 65568 | tf_op jit(solution)/shard_map/ppermute | solution.py:57
  92.4 6.1 %coarse.1 = (f32[32,32,256]{2,1,0:T(8,128)S(1)}, f32[192,256]{1,0:T(8,128)S(1)}, f32[192,256]{1,0:T(8,128)S(1)}, f32[192,256]{1,0:T(8,128)S(1)}, f32[192,256]{1,0:T(8,128)S(1)}) custom-call(f32[32,32,256]{2,1,0:T(8,128)S(1)} %get-tuple-element.49.cl_ref, f32[32,32,256]{2,1,0:T(8,128)S(1)} %get-tuple-element.50.cm_ref, ...), custom_call_target="tpu_custom_call" | custom-call | tf_op jit(solution)/shard_map/coarse/pallas_call | solution.py:478
  98.7 6.0 %collective-permute-start.17 = (f32[192,256]{1,0:T(8,128)S(1)}, f32[192,256]{1,0:T(8,128)S(1)}, u32[]{:S(2)}, u32[]{:S(2)}) collective-permute-start(f32[192,256]{1,0:T(8,128)S(1)} %get-tuple-element.71), channel_id=1, source_target_pairs={{4,0},{8,4},{12,8},{16,12},{20,16},{24,20},{28,24},{32,28},{36,32}... | collective-permute-start | bytes 589832 | tf_op jit(solution)/shard_map/ppermute | solution.py:57
  104.6 2.7 %collective-permute-start.14 = (f32[192,256]{1,0:T(8,128)S(1)}, f32[192,256]{1,0:T(8,128)S(1)}, u32[]{:S(2)}, u32[]{:S(2)}) collective-permute-start(f32[192,256]{1,0:T(8,128)S(1)} %get-tuple-element.68), channel_id=1, source_target_pairs={{0,1},{1,2},{2,3},{3,0},{4,5},{5,6},{6,7},{7,4},{8,9},{9,10},{10,1... | collective-permute-start | bytes 589832 | tf_op jit(solution)/shard_map/ppermute | solution.py:57
  107.3 1.6 %collective-permute-start.15 = (f32[192,256]{1,0:T(8,128)S(1)}, f32[192,256]{1,0:T(8,128)S(1)}, u32[]{:S(2)}, u32[]{:S(2)}) collective-permute-start(f32[192,256]{1,0:T(8,128)S(1)} %get-tuple-element.69), channel_id=1, source_target_pairs={{1,0},{2,1},{3,2},{0,3},{5,4},{6,5},{7,6},{4,7},{9,8},{10,9},{11,1... | collective-permute-start | bytes 589832 | tf_op jit(solution)/shard_map/ppermute | solution.py:57
  108.9 5.0 %collective-permute-done.16.refs_0_.n_lo = f32[192,256]{1,0:T(8,128)S(1)} collective-permute-done((f32[192,256]{1,0:T(8,128)S(1)}, f32[192,256]{1,0:T(8,128)S(1)}, u32[]{:S(2)}, u32[]{:S(2)}) %collective-permute-start.16) | collective-permute-done | bytes 196640 | tf_op jit(solution)/shard_map/ppermute | solution.py:57
  113.9 3.0 %collective-permute-start.18 = (f32[8,256]{1,0:T(8,128)S(1)}, f32[8,256]{1,0:T(8,128)S(1)}, u32[]{:S(2)}, u32[]{:S(2)}) collective-permute-start(f32[8,256]{1,0:T(8,128)S(1)} %get-tuple-element.72), channel_id=1, source_target_pairs={{0,1},{1,2},{2,3},{3,0},{4,5},{5,6},{6,7},{7,4},{8,9},{9,10},{10,1... | collective-permute-start | bytes 24584 | tf_op jit(solution)/shard_map/ppermute | solution.py:57
  118.1 1.6 %collective-permute-done.18.c_lo = f32[8,256]{1,0:T(8,128)S(1)} collective-permute-done((f32[8,256]{1,0:T(8,128)S(1)}, f32[8,256]{1,0:T(8,128)S(1)}, u32[]{:S(2)}, u32[]{:S(2)}) %collective-permute-start.18) | collective-permute-done | bytes 8224 | tf_op jit(solution)/shard_map/ppermute | solution.py:57
  119.7 1.7 %collective-permute-done.19.c_hi = f32[8,256]{1,0:T(8,128)S(1)} collective-permute-done((f32[8,256]{1,0:T(8,128)S(1)}, f32[8,256]{1,0:T(8,128)S(1)}, u32[]{:S(2)}, u32[]{:S(2)}) %collective-permute-start.19) | collective-permute-done | bytes 8224 | tf_op jit(solution)/shard_map/ppermute | solution.py:57
  121.4 10.1 %after.1 = (f32[64,64,256]{2,1,0:T(8,128)}, f32[64,64,256]{2,1,0:T(8,128)}) custom-call(f32[64,64,256]{2,1,0:T(8,128)S(1)} %get-tuple-element.48.u_ref, f32[64,64,256]{2,1,0:T(8,128)S(1)} %copy-done.2, f32[64,64,256]{2,1,0:T(8,128)} %m_ref.9, f32[32,32,256]{2,1,0:T(8,128)S(1)} %get-tuple-element.67.e_ref, f32[192,256]{1,0:T(8,128)S(1)} %collective-permute-done.14.e_lo, ...), custom_call_target="tpu_custom_call" | custom-call | tf_op jit(solution)/shard_map/after/pallas_call | solution.py:571
  (46 shorter events, 4.8 us)
Async XLA Ops:
  3.0 27.2 %copy-start = (f32[64,64,256]{2,1,0:T(8,128)S(1)}, f32[64,64,256]{2,1,0:T(8,128)}, u32[]{:S(2)}) copy-start(f32[64,64,256]{2,1,0:T(8,128)} %m_ref.9) | copy-start | bytes 12582916
  3.0 14.6 %collective-permute-start.2 = (f32[328,256]{1,0:T(8,128)}, f32[328,256]{1,0:T(8,128)S(1)}, u32[]{:S(2)}, u32[]{:S(2)}) collective-permute-start(f32[328,256]{1,0:T(8,128)} %get-tuple-element.44), channel_id=1, source_target_pairs={{0,4},{4,8},{8,12},{12,16},{16,20},{20,24},{24,28},{28,32},{32,36}... | collective-permute-start | bytes 1007624 | tf_op jit(solution)/shard_map/ppermute | solution.py:57
  3.1 14.5 %collective-permute-start.3 = (f32[328,256]{1,0:T(8,128)}, f32[328,256]{1,0:T(8,128)S(1)}, u32[]{:S(2)}, u32[]{:S(2)}) collective-permute-start(f32[328,256]{1,0:T(8,128)} %get-tuple-element.45), channel_id=1, source_target_pairs={{4,0},{8,4},{12,8},{16,12},{20,16},{24,20},{28,24},{32,28},{36,32}... | collective-permute-start | bytes 1007624 | tf_op jit(solution)/shard_map/ppermute | solution.py:57
  12.1 32.7 %collective-permute-start = (f32[328,256]{1,0:T(8,128)}, f32[328,256]{1,0:T(8,128)S(1)}, u32[]{:S(2)}, u32[]{:S(2)}) collective-permute-start(f32[328,256]{1,0:T(8,128)} %get-tuple-element.42), channel_id=1, source_target_pairs={{0,1},{1,2},{2,3},{3,0},{4,5},{5,6},{6,7},{7,4},{8,9},{9,10},{10,1... | collective-permute-start | bytes 1007624 | tf_op jit(solution)/shard_map/ppermute | solution.py:57
  15.4 29.4 %collective-permute-start.1 = (f32[328,256]{1,0:T(8,128)}, f32[328,256]{1,0:T(8,128)S(1)}, u32[]{:S(2)}, u32[]{:S(2)}) collective-permute-start(f32[328,256]{1,0:T(8,128)} %get-tuple-element.43), channel_id=1, source_target_pairs={{1,0},{2,1},{3,2},{0,3},{5,4},{6,5},{7,6},{4,7},{9,8},{10,9},{11,1... | collective-permute-start | bytes 1007624 | tf_op jit(solution)/shard_map/ppermute | solution.py:57
  17.7 27.1 %collective-permute-start.4 = (f32[16,256]{1,0:T(8,128)S(1)}, f32[16,256]{1,0:T(8,128)S(1)}, u32[]{:S(2)}, u32[]{:S(2)}) collective-permute-start(f32[16,256]{1,0:T(8,128)S(1)} %get-tuple-element.46), channel_id=1, source_target_pairs={{0,1},{1,2},{2,3},{3,0},{4,5},{5,6},{6,7},{7,4},{8,9},{9,10},{10,1... | collective-permute-start | bytes 49160 | tf_op jit(solution)/shard_map/ppermute | solution.py:57
  23.5 21.3 %collective-permute-start.5 = (f32[16,256]{1,0:T(8,128)S(1)}, f32[16,256]{1,0:T(8,128)S(1)}, u32[]{:S(2)}, u32[]{:S(2)}) collective-permute-start(f32[16,256]{1,0:T(8,128)S(1)} %get-tuple-element.47), channel_id=1, source_target_pairs={{1,0},{2,1},{3,2},{0,3},{5,4},{6,5},{7,6},{4,7},{9,8},{10,9},{11,1... | collective-permute-start | bytes 49160 | tf_op jit(solution)/shard_map/ppermute | solution.py:57
  36.3 2.8 %copy-start.4 = (f32[2,70,96,128]{3,2,1,0:T(8,128)}, f32[2,70,96,128]{3,2,1,0:T(8,128)S(1)}, u32[]{:S(2)}) copy-start(f32[2,70,96,128]{3,2,1,0:T(8,128)S(1)} %get-tuple-element.39._f) | copy-start | bytes 20643844
  39.2 2.9 %copy-start.6 = (f32[2,70,96,128]{3,2,1,0:T(8,128)}, f32[2,70,96,128]{3,2,1,0:T(8,128)S(1)}, u32[]{:S(2)}) copy-start(f32[2,70,96,128]{3,2,1,0:T(8,128)S(1)} %get-tuple-element.40._m) | copy-start | bytes 20643844
  42.0 2.7 %copy-start.8 = (f32[2,70,96,128]{3,2,1,0:T(8,128)}, f32[2,70,96,128]{3,2,1,0:T(8,128)S(1)}, u32[]{:S(2)}) copy-start(f32[2,70,96,128]{3,2,1,0:T(8,128)S(1)} %get-tuple-element.41._w) | copy-start | bytes 20643844
  44.8 3.0 %copy-start.5 = (f32[2,70,96,128]{3,2,1,0:T(8,128)S(1)}, f32[2,70,96,128]{3,2,1,0:T(8,128)}, u32[]{:S(2)}) copy-start(f32[2,70,96,128]{3,2,1,0:T(8,128)} %copy-done.4) | copy-start | bytes 20643844
  47.8 3.0 %copy-start.7 = (f32[2,70,96,128]{3,2,1,0:T(8,128)S(1)}, f32[2,70,96,128]{3,2,1,0:T(8,128)}, u32[]{:S(2)}) copy-start(f32[2,70,96,128]{3,2,1,0:T(8,128)} %copy-done.6) | copy-start | bytes 20643844
  50.7 3.0 %copy-start.9 = (f32[2,70,96,128]{3,2,1,0:T(8,128)S(1)}, f32[2,70,96,128]{3,2,1,0:T(8,128)}, u32[]{:S(2)}) copy-start(f32[2,70,96,128]{3,2,1,0:T(8,128)} %copy-done.8) | copy-start | bytes 20643844
  53.7 38.8 %copy-start.10 = (f32[128,256]{1,0:T(8,128)S(1)}, f32[128,256]{1,0:T(8,128)}, u32[]{:S(2)}) copy-start(f32[128,256]{1,0:T(8,128)} %get-tuple-element.65.knl) | copy-start | bytes 393220
  53.7 38.8 %copy-start.11 = (f32[128,256]{1,0:T(8,128)S(1)}, f32[128,256]{1,0:T(8,128)}, u32[]{:S(2)}) copy-start(f32[128,256]{1,0:T(8,128)} %get-tuple-element.66.knh) | copy-start | bytes 393220
  53.7 38.8 %copy-start.12 = (f32[128,256]{1,0:T(8,128)S(1)}, f32[128,256]{1,0:T(8,128)}, u32[]{:S(2)}) copy-start(f32[128,256]{1,0:T(8,128)} %get-tuple-element.63.kel) | copy-start | bytes 393220
  53.7 38.8 %copy-start.13 = (f32[128,256]{1,0:T(8,128)S(1)}, f32[128,256]{1,0:T(8,128)}, u32[]{:S(2)}) copy-start(f32[128,256]{1,0:T(8,128)} %get-tuple-element.64.keh) | copy-start | bytes 393220
  60.8 60.7 %copy-start.2 = (f32[64,64,256]{2,1,0:T(8,128)S(1)}, f32[64,64,256]{2,1,0:T(8,128)}, u32[]{:S(2)}) copy-start(f32[64,64,256]{2,1,0:T(8,128)} %f_ref.7) | copy-start | bytes 12582916
  60.8 22.6 %collective-permute-start.10 = (f32[384,256]{1,0:T(8,128)S(1)}, f32[384,256]{1,0:T(8,128)S(1)}, u32[]{:S(2)}, u32[]{:S(2)}) collective-permute-start(f32[384,256]{1,0:T(8,128)S(1)} %get-tuple-element.55), channel_id=1, source_target_pairs={{0,4},{4,8},{8,12},{12,16},{16,20},{20,24},{24,28},{28,32},{32,36}... | collective-permute-start | bytes 1179656 | tf_op jit(solution)/shard_map/ppermute | solution.py:57
  60.9 25.1 %collective-permute-start.11 = (f32[384,256]{1,0:T(8,128)S(1)}, f32[384,256]{1,0:T(8,128)S(1)}, u32[]{:S(2)}, u32[]{:S(2)}) collective-permute-start(f32[384,256]{1,0:T(8,128)S(1)} %get-tuple-element.56), channel_id=1, source_target_pairs={{4,0},{8,4},{12,8},{16,12},{20,16},{24,20},{28,24},{32,28},{36,32}... | collective-permute-start | bytes 1179656 | tf_op jit(solution)/shard_map/ppermute | solution.py:57
  67.7 18.8 %collective-permute-start.6 = (f32[192,256]{1,0:T(8,128)S(1)}, f32[192,256]{1,0:T(8,128)S(1)}, u32[]{:S(2)}, u32[]{:S(2)}) collective-permute-start(f32[192,256]{1,0:T(8,128)S(1)} %get-tuple-element.51), channel_id=1, source_target_pairs={{0,1},{1,2},{2,3},{3,0},{4,5},{5,6},{6,7},{7,4},{8,9},{9,10},{10,1... | collective-permute-start | bytes 589832 | tf_op jit(solution)/shard_map/ppermute | solution.py:57
  68.5 21.6 %collective-permute-start.7 = (f32[192,256]{1,0:T(8,128)S(1)}, f32[192,256]{1,0:T(8,128)S(1)}, u32[]{:S(2)}, u32[]{:S(2)}) collective-permute-start(f32[192,256]{1,0:T(8,128)S(1)} %get-tuple-element.52), channel_id=1, source_target_pairs={{1,0},{2,1},{3,2},{0,3},{5,4},{6,5},{7,6},{4,7},{9,8},{10,9},{11,1... | collective-permute-start | bytes 589832 | tf_op jit(solution)/shard_map/ppermute | solution.py:57
  71.9 18.3 %collective-permute-start.8 = (f32[192,256]{1,0:T(8,128)S(1)}, f32[192,256]{1,0:T(8,128)S(1)}, u32[]{:S(2)}, u32[]{:S(2)}) collective-permute-start(f32[192,256]{1,0:T(8,128)S(1)} %get-tuple-element.53), channel_id=1, source_target_pairs={{0,1},{1,2},{2,3},{3,0},{4,5},{5,6},{6,7},{7,4},{8,9},{9,10},{10,1... | collective-permute-start | bytes 589832 | tf_op jit(solution)/shard_map/ppermute | solution.py:57
  83.4 7.0 %collective-permute-start.9 = (f32[192,256]{1,0:T(8,128)S(1)}, f32[192,256]{1,0:T(8,128)S(1)}, u32[]{:S(2)}, u32[]{:S(2)}) collective-permute-start(f32[192,256]{1,0:T(8,128)S(1)} %get-tuple-element.54), channel_id=1, source_target_pairs={{1,0},{2,1},{3,2},{0,3},{5,4},{6,5},{7,6},{4,7},{9,8},{10,9},{11,1... | collective-permute-start | bytes 589832 | tf_op jit(solution)/shard_map/ppermute | solution.py:57
  86.0 6.5 %collective-permute-start.12 = (f32[64,256]{1,0:T(8,128)S(1)}, f32[64,256]{1,0:T(8,128)S(1)}, u32[]{:S(2)}, u32[]{:S(2)}) collective-permute-start(f32[64,256]{1,0:T(8,128)S(1)} %get-tuple-element.57), channel_id=1, source_target_pairs={{0,1},{1,2},{2,3},{3,0},{4,5},{5,6},{6,7},{7,4},{8,9},{9,10},{10,1... | collective-permute-start | bytes 196616 | tf_op jit(solution)/shard_map/ppermute | solution.py:57
  86.5 6.0 %collective-permute-start.13 = (f32[64,256]{1,0:T(8,128)S(1)}, f32[64,256]{1,0:T(8,128)S(1)}, u32[]{:S(2)}, u32[]{:S(2)}) collective-permute-start(f32[64,256]{1,0:T(8,128)S(1)} %get-tuple-element.58), channel_id=1, source_target_pairs={{1,0},{2,1},{3,2},{0,3},{5,4},{6,5},{7,6},{4,7},{9,8},{10,9},{11,1... | collective-permute-start | bytes 196616 | tf_op jit(solution)/shard_map/ppermute | solution.py:57
  98.6 15.3 %collective-permute-start.16 = (f32[192,256]{1,0:T(8,128)S(1)}, f32[192,256]{1,0:T(8,128)S(1)}, u32[]{:S(2)}, u32[]{:S(2)}) collective-permute-start(f32[192,256]{1,0:T(8,128)S(1)} %get-tuple-element.70), channel_id=1, source_target_pairs={{0,4},{4,8},{8,12},{12,16},{16,20},{20,24},{24,28},{28,32},{32,36}... | collective-permute-start | bytes 589832 | tf_op jit(solution)/shard_map/ppermute | solution.py:57
  98.7 15.2 %collective-permute-start.17 = (f32[192,256]{1,0:T(8,128)S(1)}, f32[192,256]{1,0:T(8,128)S(1)}, u32[]{:S(2)}, u32[]{:S(2)}) collective-permute-start(f32[192,256]{1,0:T(8,128)S(1)} %get-tuple-element.71), channel_id=1, source_target_pairs={{4,0},{8,4},{12,8},{16,12},{20,16},{24,20},{28,24},{32,28},{36,32}... | collective-permute-start | bytes 589832 | tf_op jit(solution)/shard_map/ppermute | solution.py:57
  104.6 13.5 %collective-permute-start.14 = (f32[192,256]{1,0:T(8,128)S(1)}, f32[192,256]{1,0:T(8,128)S(1)}, u32[]{:S(2)}, u32[]{:S(2)}) collective-permute-start(f32[192,256]{1,0:T(8,128)S(1)} %get-tuple-element.68), channel_id=1, source_target_pairs={{0,1},{1,2},{2,3},{3,0},{4,5},{5,6},{6,7},{7,4},{8,9},{9,10},{10,1... | collective-permute-start | bytes 589832 | tf_op jit(solution)/shard_map/ppermute | solution.py:57
  107.3 10.8 %collective-permute-start.15 = (f32[192,256]{1,0:T(8,128)S(1)}, f32[192,256]{1,0:T(8,128)S(1)}, u32[]{:S(2)}, u32[]{:S(2)}) collective-permute-start(f32[192,256]{1,0:T(8,128)S(1)} %get-tuple-element.69), channel_id=1, source_target_pairs={{1,0},{2,1},{3,2},{0,3},{5,4},{6,5},{7,6},{4,7},{9,8},{10,9},{11,1... | collective-permute-start | bytes 589832 | tf_op jit(solution)/shard_map/ppermute | solution.py:57
  113.9 5.8 %collective-permute-start.18 = (f32[8,256]{1,0:T(8,128)S(1)}, f32[8,256]{1,0:T(8,128)S(1)}, u32[]{:S(2)}, u32[]{:S(2)}) collective-permute-start(f32[8,256]{1,0:T(8,128)S(1)} %get-tuple-element.72), channel_id=1, source_target_pairs={{0,1},{1,2},{2,3},{3,0},{4,5},{5,6},{6,7},{7,4},{8,9},{9,10},{10,1... | collective-permute-start | bytes 24584 | tf_op jit(solution)/shard_map/ppermute | solution.py:57
  116.9 4.5 %collective-permute-start.19 = (f32[8,256]{1,0:T(8,128)S(1)}, f32[8,256]{1,0:T(8,128)S(1)}, u32[]{:S(2)}, u32[]{:S(2)}) collective-permute-start(f32[8,256]{1,0:T(8,128)S(1)} %get-tuple-element.73), channel_id=1, source_target_pairs={{1,0},{2,1},{3,2},{0,3},{5,4},{6,5},{7,6},{4,7},{9,8},{10,9},{11,1... | collective-permute-start | bytes 24584 | tf_op jit(solution)/shard_map/ppermute | solution.py:57
  (2 other events, 4.4 us)

commit v2 on v1

--- a/solution.py
+++ b/solution.py
@@ -115,8 +115,10 @@
     out[pl.ds(ENDS + 2, 6), h] = jnp.zeros((6, LANES), F32)
 
 
-def north_edges_kernel(u_ref, f_ref, m_ref, nl, nh, knl, knh, lines, line, sems):
-    copies = []
+def north_edges_kernel(
+    u_ref, f_ref, m_ref, nl, nh, knl, knh, tiles, lines, line, sems, tile_sems
+):
+    copies, tile_copies = [], []
     for side in range(2):
         for k, ref in enumerate((u_ref, f_ref, m_ref)):
             copy = pltpu.make_async_copy(
@@ -124,6 +126,16 @@
             )
             copy.start()
             copies.append(copy)
+    for side in range(2):
+        for c in range(HALVES):
+            for k, ref in enumerate((u_ref, f_ref, m_ref)):
+                copy = pltpu.make_async_copy(
+                    ref.at[:, pl.ds(side * (NX - 8), 8), half(c)],
+                    tiles.at[k, side, c],
+                    tile_sems.at[k, side, c],
+                )
+                copy.start()
+                tile_copies.append(copy)
     clear_ends(line)
     for copy in copies:
         copy.wait()
@@ -134,23 +146,12 @@
                 lambda k, d: lines[k, side, d - 1 if side == 0 else 3 - d, :, h],
                 (nl, nh)[side], (knl, knh)[side], line, h,
             )
-
-
-def east_edges_kernel(u_ref, f_ref, m_ref, el, eh, kel, keh, tiles, line, sems):
-    copies = []
-    for side in range(2):
-        for c in range(HALVES):
-            for k, ref in enumerate((u_ref, f_ref, m_ref)):
-                copy = pltpu.make_async_copy(
-                    ref.at[:, pl.ds(side * (NX - 8), 8), half(c)],
-                    tiles.at[k, side, c],
-                    sems.at[k, side, c],
-                )
-                copy.start()
-                copies.append(copy)
+    for copy in tile_copies:
+        copy.wait()
+
+
+def east_edges_kernel(tiles, el, eh, kel, keh, line):
     clear_ends(line)
-    for copy in copies:
-        copy.wait()
     for side in range(2):
         for c in range(HALVES):
 
@@ -161,19 +162,37 @@
             write_strip(get, (el, eh)[side], (kel, keh)[side], line, half(c))
 
 
-def edges(kernel, buffer, sems, u, f, m):
-    return pl.pallas_call(
-        kernel,
-        out_shape=(shape(STRIP, NC),) * 2 + (shape(2 * SLOT, NC),) * 2,
+STRIPS = (shape(STRIP, NC),) * 2 + (shape(2 * SLOT, NC),) * 2
+TILES = (3, 2, HALVES, NY, 8, LANES)
+
+
+def north_edges(u, f, m):
+    return pl.pallas_call(
+        north_edges_kernel,
+        out_shape=STRIPS + (shape(*TILES),),
         in_specs=[IN_HBM] * 3,
+        out_specs=(IN_VMEM,) * 5,
+        scratch_shapes=[
+            VMEM((3, 2, 3, NX, NC), F32),
+            VMEM((SLOT + 16, LANES), F32),
+            pltpu.SemaphoreType.DMA((3, 2)),
+            pltpu.SemaphoreType.DMA((3, 2, HALVES)),
+        ],
+        compiler_params=pltpu.CompilerParams(vmem_limit_bytes=48 * 2**20),
+        name="north_edges",
+    )(u, f, m)
+
+
+def east_edges(tiles):
+    return pl.pallas_call(
+        east_edges_kernel,
+        out_shape=STRIPS,
+        in_specs=[IN_VMEM],
         out_specs=(IN_VMEM,) * 4,
-        scratch_shapes=[
-            VMEM(buffer, F32),
-            VMEM((SLOT + 16, LANES), F32),
-            pltpu.SemaphoreType.DMA(sems),
-        ],
-        compiler_params=pltpu.CompilerParams(vmem_limit_bytes=58 * 2**20),
-    )(u, f, m)
+        scratch_shapes=[VMEM((SLOT + 16, LANES), F32)],
+        compiler_params=pltpu.CompilerParams(vmem_limit_bytes=8 * 2**20),
+        name="east_edges",
+    )(tiles)
 
 
 def mass_kernel(m_ref, low, high, tiles, pair, sems):
@@ -403,7 +422,7 @@
         out_specs=(IN_VMEM,) * 15,
         input_output_aliases={k: k for k in range(4)},
         scratch_shapes=[VMEM((FY, FX, LANES), F32), VMEM((2, 2, NX, LANES), F32)],
-        compiler_params=pltpu.CompilerParams(vmem_limit_bytes=7 * 2**20),
+        compiler_params=pltpu.CompilerParams(vmem_limit_bytes=9 * 2**20),
         name="before",
     )(*padded, *strips)
 
@@ -482,7 +501,7 @@
         out_specs=(IN_VMEM,) * 5,
         scratch_shapes=[VMEM((GY, GX, LANES), F32)] * 4
         + [VMEM((NY, LANES), F32), VMEM((SLOT + 16, LANES), F32)],
-        compiler_params=pltpu.CompilerParams(vmem_limit_bytes=7 * 2**20),
+        compiler_params=pltpu.CompilerParams(vmem_limit_bytes=9 * 2**20),
         name="coarse",
     )(right, mass, *mass_strips, *strips, *u_strips, *kept)
 
@@ -586,9 +605,9 @@
 
 def body(right_side, first_guess, mass_term):
     f, u, m = right_side, first_guess, mass_term
-    nl, nh, *north_kept = edges(north_edges_kernel, (3, 2, 3, NX, NC), (3, 2), u, f, m)
-    el, eh, *kept = edges(east_edges_kernel, (3, 2, HALVES, NY, 8, LANES), (3, 2, HALVES), u, f, m)
-    kept += north_kept
+    nl, nh, knl, knh, tiles = north_edges(u, f, m)
+    el, eh, *kept = east_edges(tiles)
+    kept += [knl, knh]
     old = halos(FINE_CELLS, NX, el, eh, nl, nh)
     columns = mass_columns(m)
     padded = load(u, f, m)

time: 132 us -> 111 us (0.84)
  the two profiles are of different devices: /device:TPU:32 before, /device:TPU:31 now
where the time goes in v2:
time: 111 us
  waiting for transfers between devices  41.6 us (37%)
  starting transfers between devices  39.6 us (36%)
  Pallas kernels  28.7 us (26%)
    ppermute x20, waiting for transfers between devices, exchange(): return (lax.ppermute(high, axis, up), lax.ppermute(low, axis, down))  41.6 us
    ppermute x20, starting transfers between devices, exchange(): return (lax.ppermute(high, axis, up), lax.ppermute(low, axis, down))  39.6 us
    pallas_call x1, Pallas kernels, after(): pl.pallas_call(after_kernel, out_shape=(shape(NY, NX, NC),) * 2, in_specs...  10.1 us
    pallas_call x1, Pallas kernels, before(): pl.pallas_call(before_kernel, out_shape=(shape(*PADDED),) * 4 + (shape(NY...  7.07 us
    pallas_call x1, Pallas kernels, coarse(): pl.pallas_call(coarse_kernel, out_shape=(shape(CY, CX, NC),) + (shape(3 *...  6.12 us
    pallas_call x1, Pallas kernels, north_edges(): pl.pallas_call(north_edges_kernel, out_shape=STRIPS + (shape(*TILES),), i...  2.55 us
  transfers between devices with their start and end apart: 20, of which 10 were waited for; matrix products, arithmetic and copies ran while one was open for 0% of the time, Pallas kernels for 3%

profile of v2, /device:TPU:31, one launch (start us, length us, event | category | flops | bytes accessed | tf_op | source)
XLA Modules:
  0.0 111.0 jit_solution(12834117183126447672)
XLA Ops:
  0.7 2.6 %north_edges.1 = (f32[328,256]{1,0:T(8,128)S(1)}, f32[328,256]{1,0:T(8,128)S(1)}, f32[128,256]{1,0:T(8,128)S(1)}, f32[128,256]{1,0:T(8,128)S(1)}, f32[3,2,2,64,8,128]{5,4,3,2,1,0:T(8,128)S(1)}) custom-call(f32[64,64,256]{2,1,0:T(8,128)} %u_ref.3, f32[64,64,256]{2,1,0:T(8,128)} %f_ref.5, f32[64,64,256]{2,1,0:T(8,128)} %m_ref.7), custom_call_target="tpu_custom_call" | custom-call | tf_op jit(solution)/shard_map/north_edges/pallas_call | solution.py:170
  3.2 1.8 %collective-permute-start.2 = (f32[328,256]{1,0:T(8,128)S(1)}, f32[328,256]{1,0:T(8,128)S(1)}, u32[]{:S(2)}, u32[]{:S(2)}) collective-permute-start(f32[328,256]{1,0:T(8,128)S(1)} %get-tuple-element.46), channel_id=1, source_target_pairs={{0,4},{4,8},{8,12},{12,16},{16,20},{20,24},{24,28},{28,32},{32,36}... | collective-permute-start | bytes 1007624 | tf_op jit(solution)/shard_map/ppermute | solution.py:57
  5.1 0.2 east_edges.1
  5.3 3.1 %collective-permute-start = (f32[328,256]{1,0:T(8,128)S(1)}, f32[328,256]{1,0:T(8,128)S(1)}, u32[]{:S(2)}, u32[]{:S(2)}) collective-permute-start(f32[328,256]{1,0:T(8,128)S(1)} %get-tuple-element.44), channel_id=1, source_target_pairs={{0,1},{1,2},{2,3},{3,0},{4,5},{5,6},{6,7},{7,4},{8,9},{9,10},{10,1... | collective-permute-start | bytes 1007624 | tf_op jit(solution)/shard_map/ppermute | solution.py:57
  8.4 2.2 %collective-permute-start.1 = (f32[328,256]{1,0:T(8,128)S(1)}, f32[328,256]{1,0:T(8,128)S(1)}, u32[]{:S(2)}, u32[]{:S(2)}) collective-permute-start(f32[328,256]{1,0:T(8,128)S(1)} %get-tuple-element.45), channel_id=1, source_target_pairs={{1,0},{2,1},{3,2},{0,3},{5,4},{6,5},{7,6},{4,7},{9,8},{10,9},{11,1... | collective-permute-start | bytes 1007624 | tf_op jit(solution)/shard_map/ppermute | solution.py:57
  10.6 15.8 %collective-permute-done.3.refs_1_.n_hi.h_nh = f32[328,256]{1,0:T(8,128)S(1)} collective-permute-done((f32[328,256]{1,0:T(8,128)S(1)}, f32[328,256]{1,0:T(8,128)S(1)}, u32[]{:S(2)}, u32[]{:S(2)}) %collective-permute-start.3) | collective-permute-done | bytes 335904 | tf_op jit(solution)/shard_map/ppermute | solution.py:57
  26.4 2.3 %collective-permute-start.4 = (f32[16,256]{1,0:T(8,128)S(1)}, f32[16,256]{1,0:T(8,128)S(1)}, u32[]{:S(2)}, u32[]{:S(2)}) collective-permute-start(f32[16,256]{1,0:T(8,128)S(1)} %get-tuple-element.48), channel_id=1, source_target_pairs={{0,1},{1,2},{2,3},{3,0},{4,5},{5,6},{6,7},{7,4},{8,9},{9,10},{10,1... | collective-permute-start | bytes 49160 | tf_op jit(solution)/shard_map/ppermute | solution.py:57
  28.7 1.4 %collective-permute-start.5 = (f32[16,256]{1,0:T(8,128)S(1)}, f32[16,256]{1,0:T(8,128)S(1)}, u32[]{:S(2)}, u32[]{:S(2)}) collective-permute-start(f32[16,256]{1,0:T(8,128)S(1)} %get-tuple-element.49), channel_id=1, source_target_pairs={{1,0},{2,1},{3,2},{0,3},{5,4},{6,5},{7,6},{4,7},{9,8},{10,9},{11,1... | collective-permute-start | bytes 49160 | tf_op jit(solution)/shard_map/ppermute | solution.py:57
  30.1 1.7 %load.1 = (f32[2,70,96,128]{3,2,1,0:T(8,128)S(1)}, f32[2,70,96,128]{3,2,1,0:T(8,128)S(1)}, f32[2,70,96,128]{3,2,1,0:T(8,128)S(1)}, f32[2,70,96,128]{3,2,1,0:T(8,128)S(1)}) custom-call(f32[64,64,256]{2,1,0:T(8,128)S(1)} %copy-done.2, f32[64,64,256]{2,1,0:T(8,128)S(1)} %copy-done.1, f32[64,64,256]{2,1,0:T(8,128)S(1)} %copy-done), custom_call_target="tpu_custom_call" | custom-call | flops 67108864 | bytes 12582912 | tf_op jit(solution)/shard_map/load/pallas_call | solution.py:345
  31.9 0.0 copy-start.5
  31.9 0.9 collective-permute-done.5.c_hi.h_ch
  32.8 7.1 %before.1 = (f32[2,70,96,128]{3,2,1,0:T(8,128)S(1)}, f32[2,70,96,128]{3,2,1,0:T(8,128)S(1)}, f32[2,70,96,128]{3,2,1,0:T(8,128)S(1)}, f32[2,70,96,128]{3,2,1,0:T(...) custom-call(f32[2,70,96,128]{3,2,1,0:T(8,128)S(1)} %get-tuple-elemen, ...), custom_call_target="tpu_custom_call", output_to_operand_aliasing={{0}: (0, {}), {1}: (1, {}), {2}: (2, {}), {3}: (3, {})} | custom-call | tf_op jit(solution)/shard_map/before/pallas_call | solution.py:413
  39.9 1.1 collective-permute-start.10
  41.0 0.9 mass_columns.1
  41.9 3.9 %collective-permute-start.6 = (f32[192,256]{1,0:T(8,128)S(1)}, f32[192,256]{1,0:T(8,128)S(1)}, u32[]{:S(2)}, u32[]{:S(2)}) collective-permute-start(f32[192,256]{1,0:T(8,128)S(1)} %get-tuple-element.53), channel_id=1, source_target_pairs={{0,1},{1,2},{2,3},{3,0},{4,5},{5,6},{6,7},{7,4},{8,9},{9,10},{10,1... | collective-permute-start | bytes 589832 | tf_op jit(solution)/shard_map/ppermute | solution.py:57
  45.8 2.4 %collective-permute-start.8 = (f32[192,256]{1,0:T(8,128)S(1)}, f32[192,256]{1,0:T(8,128)S(1)}, u32[]{:S(2)}, u32[]{:S(2)}) collective-permute-start(f32[192,256]{1,0:T(8,128)S(1)} %get-tuple-element.55), channel_id=1, source_target_pairs={{0,1},{1,2},{2,3},{3,0},{4,5},{5,6},{6,7},{7,4},{8,9},{9,10},{10,1... | collective-permute-start | bytes 589832 | tf_op jit(solution)/shard_map/ppermute | solution.py:57
  48.2 7.7 %collective-permute-done.10.refs_0_.n_lo = f32[384,256]{1,0:T(8,128)S(1)} collective-permute-done((f32[384,256]{1,0:T(8,128)S(1)}, f32[384,256]{1,0:T(8,128)S(1)}, u32[]{:S(2)}, u32[]{:S(2)}) %collective-permute-start.10) | collective-permute-done | bytes 393248 | tf_op jit(solution)/shard_map/ppermute | solution.py:57
  55.9 4.5 %collective-permute-start.9 = (f32[192,256]{1,0:T(8,128)S(1)}, f32[192,256]{1,0:T(8,128)S(1)}, u32[]{:S(2)}, u32[]{:S(2)}) collective-permute-start(f32[192,256]{1,0:T(8,128)S(1)} %get-tuple-element.56), channel_id=1, source_target_pairs={{1,0},{2,1},{3,2},{0,3},{5,4},{6,5},{7,6},{4,7},{9,8},{10,9},{11,1... | collective-permute-start | bytes 589832 | tf_op jit(solution)/shard_map/ppermute | solution.py:57
  60.4 4.6 %collective-permute-done.11.refs_1_.n_hi = f32[384,256]{1,0:T(8,128)S(1)} collective-permute-done((f32[384,256]{1,0:T(8,128)S(1)}, f32[384,256]{1,0:T(8,128)S(1)}, u32[]{:S(2)}, u32[]{:S(2)}) %collective-permute-start.11) | collective-permute-done | bytes 393248 | tf_op jit(solution)/shard_map/ppermute | solution.py:57
  65.1 2.3 %collective-permute-start.12 = (f32[64,256]{1,0:T(8,128)S(1)}, f32[64,256]{1,0:T(8,128)S(1)}, u32[]{:S(2)}, u32[]{:S(2)}) collective-permute-start(f32[64,256]{1,0:T(8,128)S(1)} %get-tuple-element.59), channel_id=1, source_target_pairs={{0,1},{1,2},{2,3},{3,0},{4,5},{5,6},{6,7},{7,4},{8,9},{9,10},{10,1... | collective-permute-start | bytes 196616 | tf_op jit(solution)/shard_map/ppermute | solution.py:57
  67.5 1.3 %collective-permute-start.13 = (f32[64,256]{1,0:T(8,128)S(1)}, f32[64,256]{1,0:T(8,128)S(1)}, u32[]{:S(2)}, u32[]{:S(2)}) collective-permute-start(f32[64,256]{1,0:T(8,128)S(1)} %get-tuple-element.60), channel_id=1, source_target_pairs={{1,0},{2,1},{3,2},{0,3},{5,4},{6,5},{7,6},{4,7},{9,8},{10,9},{11,1... | collective-permute-start | bytes 196616 | tf_op jit(solution)/shard_map/ppermute | solution.py:57
  68.8 1.6 %collective-permute-done.12.c_lo = f32[64,256]{1,0:T(8,128)S(1)} collective-permute-done((f32[64,256]{1,0:T(8,128)S(1)}, f32[64,256]{1,0:T(8,128)S(1)}, u32[]{:S(2)}, u32[]{:S(2)}) %collective-permute-start.12) | collective-permute-done | bytes 65568 | tf_op jit(solution)/shard_map/ppermute | solution.py:57
  70.4 1.0 collective-permute-done.13.c_hi
  71.5 6.1 %coarse.1 = (f32[32,32,256]{2,1,0:T(8,128)S(1)}, f32[192,256]{1,0:T(8,128)S(1)}, f32[192,256]{1,0:T(8,128)S(1)}, f32[192,256]{1,0:T(8,128)S(1)}, f32[192,256]{1,0:T(8,128)S(1)}) custom-call(f32[32,32,256]{2,1,0:T(8,128)S(1)} %get-tuple-element.51.cl_ref, f32[32,32,256]{2,1,0:T(8,128)S(1)} %get-tuple-element.52.cm_ref, ...), custom_call_target="tpu_custom_call" | custom-call | tf_op jit(solution)/shard_map/coarse/pallas_call | solution.py:497
  77.6 4.4 %collective-permute-start.16 = (f32[192,256]{1,0:T(8,128)S(1)}, f32[192,256]{1,0:T(8,128)S(1)}, u32[]{:S(2)}, u32[]{:S(2)}) collective-permute-start(f32[192,256]{1,0:T(8,128)S(1)} %get-tuple-element.72), channel_id=1, source_target_pairs={{0,4},{4,8},{8,12},{12,16},{16,20},{20,24},{24,28},{28,32},{32,36}... | collective-permute-start | bytes 589832 | tf_op jit(solution)/shard_map/ppermute | solution.py:57
  82.0 3.8 %collective-permute-start.14 = (f32[192,256]{1,0:T(8,128)S(1)}, f32[192,256]{1,0:T(8,128)S(1)}, u32[]{:S(2)}, u32[]{:S(2)}) collective-permute-start(f32[192,256]{1,0:T(8,128)S(1)} %get-tuple-element.70), channel_id=1, source_target_pairs={{0,1},{1,2},{2,3},{3,0},{4,5},{5,6},{6,7},{7,4},{8,9},{9,10},{10,1... | collective-permute-start | bytes 589832 | tf_op jit(solution)/shard_map/ppermute | solution.py:57
  85.9 3.3 %collective-permute-done.16.refs_0_.n_lo = f32[192,256]{1,0:T(8,128)S(1)} collective-permute-done((f32[192,256]{1,0:T(8,128)S(1)}, f32[192,256]{1,0:T(8,128)S(1)}, u32[]{:S(2)}, u32[]{:S(2)}) %collective-permute-start.16) | collective-permute-done | bytes 196640 | tf_op jit(solution)/shard_map/ppermute | solution.py:57
  89.2 3.1 %collective-permute-done.17.refs_1_.n_hi = f32[192,256]{1,0:T(8,128)S(1)} collective-permute-done((f32[192,256]{1,0:T(8,128)S(1)}, f32[192,256]{1,0:T(8,128)S(1)}, u32[]{:S(2)}, u32[]{:S(2)}) %collective-permute-start.17) | collective-permute-done | bytes 196640 | tf_op jit(solution)/shard_map/ppermute | solution.py:57
  92.3 5.1 %collective-permute-start.18 = (f32[8,256]{1,0:T(8,128)S(1)}, f32[8,256]{1,0:T(8,128)S(1)}, u32[]{:S(2)}, u32[]{:S(2)}) collective-permute-start(f32[8,256]{1,0:T(8,128)S(1)} %get-tuple-element.74), channel_id=1, source_target_pairs={{0,1},{1,2},{2,3},{3,0},{4,5},{5,6},{6,7},{7,4},{8,9},{9,10},{10,1... | collective-permute-start | bytes 24584 | tf_op jit(solution)/shard_map/ppermute | solution.py:57
  97.4 0.8 collective-permute-done.18.c_lo
  98.1 2.6 %collective-permute-done.19.c_hi = f32[8,256]{1,0:T(8,128)S(1)} collective-permute-done((f32[8,256]{1,0:T(8,128)S(1)}, f32[8,256]{1,0:T(8,128)S(1)}, u32[]{:S(2)}, u32[]{:S(2)}) %collective-permute-start.19) | collective-permute-done | bytes 8224 | tf_op jit(solution)/shard_map/ppermute | solution.py:57
  100.8 10.1 %after.1 = (f32[64,64,256]{2,1,0:T(8,128)}, f32[64,64,256]{2,1,0:T(8,128)}) custom-call(f32[64,64,256]{2,1,0:T(8,128)S(1)} %get-tuple-element.50.u_ref, f32[64,64,256]{2,1,0:T(8,128)S(1)} %copy-done.1, f32[64,64,256]{2,1,0:T(8,128)} %m_ref.7, f32[32,32,256]{2,1,0:T(8,128)S(1)} %get-tuple-element.69.e_ref, f32[192,256]{1,0:T(8,128)S(1)} %collective-permute-done.14.e_lo, ...), custom_call_target="tpu_custom_call" | custom-call | tf_op jit(solution)/shard_map/after/pallas_call | solution.py:590
  (40 shorter events, 0.1 us)
Async XLA Ops:
  0.6 29.5 %copy-start.1 = (f32[64,64,256]{2,1,0:T(8,128)S(1)}, f32[64,64,256]{2,1,0:T(8,128)}, u32[]{:S(2)}) copy-start(f32[64,64,256]{2,1,0:T(8,128)} %f_ref.5) | copy-start | bytes 12582916
  0.6 29.5 %copy-start.2 = (f32[64,64,256]{2,1,0:T(8,128)S(1)}, f32[64,64,256]{2,1,0:T(8,128)}, u32[]{:S(2)}) copy-start(f32[64,64,256]{2,1,0:T(8,128)} %u_ref.3) | copy-start | bytes 12582916
  0.6 29.4 %copy-start = (f32[64,64,256]{2,1,0:T(8,128)S(1)}, f32[64,64,256]{2,1,0:T(8,128)}, u32[]{:S(2)}) copy-start(f32[64,64,256]{2,1,0:T(8,128)} %m_ref.7) | copy-start | bytes 12582916
  3.2 28.6 %copy-start.7 = (f32[128,256]{1,0:T(8,128)}, f32[128,256]{1,0:T(8,128)S(1)}, u32[]{:S(2)}) copy-start(f32[128,256]{1,0:T(8,128)S(1)} %get-tuple-element.67.knl) | copy-start | bytes 393220
  3.2 28.6 %copy-start.9 = (f32[128,256]{1,0:T(8,128)}, f32[128,256]{1,0:T(8,128)S(1)}, u32[]{:S(2)}) copy-start(f32[128,256]{1,0:T(8,128)S(1)} %get-tuple-element.68.knh) | copy-start | bytes 393220
  3.2 7.3 %collective-permute-start.2 = (f32[328,256]{1,0:T(8,128)S(1)}, f32[328,256]{1,0:T(8,128)S(1)}, u32[]{:S(2)}, u32[]{:S(2)}) collective-permute-start(f32[328,256]{1,0:T(8,128)S(1)} %get-tuple-element.46), channel_id=1, source_target_pairs={{0,4},{4,8},{8,12},{12,16},{16,20},{20,24},{24,28},{28,32},{32,36}... | collective-permute-start | bytes 1007624 | tf_op jit(solution)/shard_map/ppermute | solution.py:57
  5.1 21.3 %collective-permute-start.3 = (f32[328,256]{1,0:T(8,128)S(1)}, f32[328,256]{1,0:T(8,128)S(1)}, u32[]{:S(2)}, u32[]{:S(2)}) collective-permute-start(f32[328,256]{1,0:T(8,128)S(1)} %get-tuple-element.47), channel_id=1, source_target_pairs={{4,0},{8,4},{12,8},{16,12},{20,16},{24,20},{28,24},{32,28},{36,32}... | collective-permute-start | bytes 1007624 | tf_op jit(solution)/shard_map/ppermute | solution.py:57
  5.3 26.6 %collective-permute-start = (f32[328,256]{1,0:T(8,128)S(1)}, f32[328,256]{1,0:T(8,128)S(1)}, u32[]{:S(2)}, u32[]{:S(2)}) collective-permute-start(f32[328,256]{1,0:T(8,128)S(1)} %get-tuple-element.44), channel_id=1, source_target_pairs={{0,1},{1,2},{2,3},{3,0},{4,5},{5,6},{6,7},{7,4},{8,9},{9,10},{10,1... | collective-permute-start | bytes 1007624 | tf_op jit(solution)/shard_map/ppermute | solution.py:57
  8.4 23.5 %collective-permute-start.1 = (f32[328,256]{1,0:T(8,128)S(1)}, f32[328,256]{1,0:T(8,128)S(1)}, u32[]{:S(2)}, u32[]{:S(2)}) collective-permute-start(f32[328,256]{1,0:T(8,128)S(1)} %get-tuple-element.45), channel_id=1, source_target_pairs={{1,0},{2,1},{3,2},{0,3},{5,4},{6,5},{7,6},{4,7},{9,8},{10,9},{11,1... | collective-permute-start | bytes 1007624 | tf_op jit(solution)/shard_map/ppermute | solution.py:57
  26.4 13.5 %copy-start.3 = (f32[328,256]{1,0:T(8,128)}, f32[328,256]{1,0:T(8,128)S(1)}, u32[]{:S(2)}) copy-start(f32[328,256]{1,0:T(8,128)S(1)} %collective-permute-done.3.refs_1_.n_hi.h_nh) | copy-start | bytes 1007620
  26.4 5.5 %collective-permute-start.4 = (f32[16,256]{1,0:T(8,128)S(1)}, f32[16,256]{1,0:T(8,128)S(1)}, u32[]{:S(2)}, u32[]{:S(2)}) collective-permute-start(f32[16,256]{1,0:T(8,128)S(1)} %get-tuple-element.48), channel_id=1, source_target_pairs={{0,1},{1,2},{2,3},{3,0},{4,5},{5,6},{6,7},{7,4},{8,9},{9,10},{10,1... | collective-permute-start | bytes 49160 | tf_op jit(solution)/shard_map/ppermute | solution.py:57
  28.7 4.1 %collective-permute-start.5 = (f32[16,256]{1,0:T(8,128)S(1)}, f32[16,256]{1,0:T(8,128)S(1)}, u32[]{:S(2)}, u32[]{:S(2)}) collective-permute-start(f32[16,256]{1,0:T(8,128)S(1)} %get-tuple-element.49), channel_id=1, source_target_pairs={{1,0},{2,1},{3,2},{0,3},{5,4},{6,5},{7,6},{4,7},{9,8},{10,9},{11,1... | collective-permute-start | bytes 49160 | tf_op jit(solution)/shard_map/ppermute | solution.py:57
  31.9 8.0 %copy-start.5 = (f32[328,256]{1,0:T(8,128)}, f32[328,256]{1,0:T(8,128)S(1)}, u32[]{:S(2)}) copy-start(f32[328,256]{1,0:T(8,128)S(1)} %collective-permute-done.e_lo.h_el) | copy-start | bytes 1007620
  32.8 38.7 %copy-start.8 = (f32[128,256]{1,0:T(8,128)S(1)}, f32[128,256]{1,0:T(8,128)}, u32[]{:S(2)}) copy-start(f32[128,256]{1,0:T(8,128)} %copy-done.7) | copy-start | bytes 393220
  32.8 38.7 %copy-start.10 = (f32[128,256]{1,0:T(8,128)S(1)}, f32[128,256]{1,0:T(8,128)}, u32[]{:S(2)}) copy-start(f32[128,256]{1,0:T(8,128)} %copy-done.9) | copy-start | bytes 393220
  39.9 60.8 %copy-start.4 = (f32[328,256]{1,0:T(8,128)S(1)}, f32[328,256]{1,0:T(8,128)}, u32[]{:S(2)}) copy-start(f32[328,256]{1,0:T(8,128)} %copy-done.3) | copy-start | bytes 1007620
  39.9 60.8 %copy-start.6 = (f32[328,256]{1,0:T(8,128)S(1)}, f32[328,256]{1,0:T(8,128)}, u32[]{:S(2)}) copy-start(f32[328,256]{1,0:T(8,128)} %copy-done.5) | copy-start | bytes 1007620
  39.9 16.0 %collective-permute-start.10 = (f32[384,256]{1,0:T(8,128)S(1)}, f32[384,256]{1,0:T(8,128)S(1)}, u32[]{:S(2)}, u32[]{:S(2)}) collective-permute-start(f32[384,256]{1,0:T(8,128)S(1)} %get-tuple-element.57), channel_id=1, source_target_pairs={{0,4},{4,8},{8,12},{12,16},{16,20},{20,24},{24,28},{28,32},{32,36}... | collective-permute-start | bytes 1179656 | tf_op jit(solution)/shard_map/ppermute | solution.py:57
  41.0 24.1 %collective-permute-start.11 = (f32[384,256]{1,0:T(8,128)S(1)}, f32[384,256]{1,0:T(8,128)S(1)}, u32[]{:S(2)}, u32[]{:S(2)}) collective-permute-start(f32[384,256]{1,0:T(8,128)S(1)} %get-tuple-element.58), channel_id=1, source_target_pairs={{4,0},{8,4},{12,8},{16,12},{20,16},{24,20},{28,24},{32,28},{36,32}... | collective-permute-start | bytes 1179656 | tf_op jit(solution)/shard_map/ppermute | solution.py:57
  41.9 25.6 %collective-permute-start.6 = (f32[192,256]{1,0:T(8,128)S(1)}, f32[192,256]{1,0:T(8,128)S(1)}, u32[]{:S(2)}, u32[]{:S(2)}) collective-permute-start(f32[192,256]{1,0:T(8,128)S(1)} %get-tuple-element.53), channel_id=1, source_target_pairs={{0,1},{1,2},{2,3},{3,0},{4,5},{5,6},{6,7},{7,4},{8,9},{9,10},{10,1... | collective-permute-start | bytes 589832 | tf_op jit(solution)/shard_map/ppermute | solution.py:57
  45.8 23.0 %collective-permute-start.7 = (f32[192,256]{1,0:T(8,128)S(1)}, f32[192,256]{1,0:T(8,128)S(1)}, u32[]{:S(2)}, u32[]{:S(2)}) collective-permute-start(f32[192,256]{1,0:T(8,128)S(1)} %get-tuple-element.54), channel_id=1, source_target_pairs={{1,0},{2,1},{3,2},{0,3},{5,4},{6,5},{7,6},{4,7},{9,8},{10,9},{11,1... | collective-permute-start | bytes 589832 | tf_op jit(solution)/shard_map/ppermute | solution.py:57
  45.8 23.0 %collective-permute-start.8 = (f32[192,256]{1,0:T(8,128)S(1)}, f32[192,256]{1,0:T(8,128)S(1)}, u32[]{:S(2)}, u32[]{:S(2)}) collective-permute-start(f32[192,256]{1,0:T(8,128)S(1)} %get-tuple-element.55), channel_id=1, source_target_pairs={{0,1},{1,2},{2,3},{3,0},{4,5},{5,6},{6,7},{7,4},{8,9},{9,10},{10,1... | collective-permute-start | bytes 589832 | tf_op jit(solution)/shard_map/ppermute | solution.py:57
  55.9 12.9 %collective-permute-start.9 = (f32[192,256]{1,0:T(8,128)S(1)}, f32[192,256]{1,0:T(8,128)S(1)}, u32[]{:S(2)}, u32[]{:S(2)}) collective-permute-start(f32[192,256]{1,0:T(8,128)S(1)} %get-tuple-element.56), channel_id=1, source_target_pairs={{1,0},{2,1},{3,2},{0,3},{5,4},{6,5},{7,6},{4,7},{9,8},{10,9},{11,1... | collective-permute-start | bytes 589832 | tf_op jit(solution)/shard_map/ppermute | solution.py:57
  65.1 5.3 %collective-permute-start.12 = (f32[64,256]{1,0:T(8,128)S(1)}, f32[64,256]{1,0:T(8,128)S(1)}, u32[]{:S(2)}, u32[]{:S(2)}) collective-permute-start(f32[64,256]{1,0:T(8,128)S(1)} %get-tuple-element.59), channel_id=1, source_target_pairs={{0,1},{1,2},{2,3},{3,0},{4,5},{5,6},{6,7},{7,4},{8,9},{9,10},{10,1... | collective-permute-start | bytes 196616 | tf_op jit(solution)/shard_map/ppermute | solution.py:57
  67.5 4.0 %collective-permute-start.13 = (f32[64,256]{1,0:T(8,128)S(1)}, f32[64,256]{1,0:T(8,128)S(1)}, u32[]{:S(2)}, u32[]{:S(2)}) collective-permute-start(f32[64,256]{1,0:T(8,128)S(1)} %get-tuple-element.60), channel_id=1, source_target_pairs={{1,0},{2,1},{3,2},{0,3},{5,4},{6,5},{7,6},{4,7},{9,8},{10,9},{11,1... | collective-permute-start | bytes 196616 | tf_op jit(solution)/shard_map/ppermute | solution.py:57
  77.6 11.5 %collective-permute-start.16 = (f32[192,256]{1,0:T(8,128)S(1)}, f32[192,256]{1,0:T(8,128)S(1)}, u32[]{:S(2)}, u32[]{:S(2)}) collective-permute-start(f32[192,256]{1,0:T(8,128)S(1)} %get-tuple-element.72), channel_id=1, source_target_pairs={{0,4},{4,8},{8,12},{12,16},{16,20},{20,24},{24,28},{28,32},{32,36}... | collective-permute-start | bytes 589832 | tf_op jit(solution)/shard_map/ppermute | solution.py:57
  82.0 10.3 %collective-permute-start.17 = (f32[192,256]{1,0:T(8,128)S(1)}, f32[192,256]{1,0:T(8,128)S(1)}, u32[]{:S(2)}, u32[]{:S(2)}) collective-permute-start(f32[192,256]{1,0:T(8,128)S(1)} %get-tuple-element.73), channel_id=1, source_target_pairs={{4,0},{8,4},{12,8},{16,12},{20,16},{24,20},{28,24},{32,28},{36,32}... | collective-permute-start | bytes 589832 | tf_op jit(solution)/shard_map/ppermute | solution.py:57
  82.0 15.3 %collective-permute-start.14 = (f32[192,256]{1,0:T(8,128)S(1)}, f32[192,256]{1,0:T(8,128)S(1)}, u32[]{:S(2)}, u32[]{:S(2)}) collective-permute-start(f32[192,256]{1,0:T(8,128)S(1)} %get-tuple-element.70), channel_id=1, source_target_pairs={{0,1},{1,2},{2,3},{3,0},{4,5},{5,6},{6,7},{7,4},{8,9},{9,10},{10,1... | collective-permute-start | bytes 589832 | tf_op jit(solution)/shard_map/ppermute | solution.py:57
  85.9 11.5 %collective-permute-start.15 = (f32[192,256]{1,0:T(8,128)S(1)}, f32[192,256]{1,0:T(8,128)S(1)}, u32[]{:S(2)}, u32[]{:S(2)}) collective-permute-start(f32[192,256]{1,0:T(8,128)S(1)} %get-tuple-element.71), channel_id=1, source_target_pairs={{1,0},{2,1},{3,2},{0,3},{5,4},{6,5},{7,6},{4,7},{9,8},{10,9},{11,1... | collective-permute-start | bytes 589832 | tf_op jit(solution)/shard_map/ppermute | solution.py:57
  92.3 5.9 %collective-permute-start.18 = (f32[8,256]{1,0:T(8,128)S(1)}, f32[8,256]{1,0:T(8,128)S(1)}, u32[]{:S(2)}, u32[]{:S(2)}) collective-permute-start(f32[8,256]{1,0:T(8,128)S(1)} %get-tuple-element.74), channel_id=1, source_target_pairs={{0,1},{1,2},{2,3},{3,0},{4,5},{5,6},{6,7},{7,4},{8,9},{9,10},{10,1... | collective-permute-start | bytes 24584 | tf_op jit(solution)/shard_map/ppermute | solution.py:57
  97.4 3.4 %collective-permute-start.19 = (f32[8,256]{1,0:T(8,128)S(1)}, f32[8,256]{1,0:T(8,128)S(1)}, u32[]{:S(2)}, u32[]{:S(2)}) collective-permute-start(f32[8,256]{1,0:T(8,128)S(1)} %get-tuple-element.75), channel_id=1, source_target_pairs={{1,0},{2,1},{3,2},{0,3},{5,4},{6,5},{7,6},{4,7},{9,8},{10,9},{11,1... | collective-permute-start | bytes 24584 | tf_op jit(solution)/shard_map/ppermute | solution.py:57
